TPU v7x, 16 devices: a whole 2x2x2 slice. The times are simulated.
16 devices in a mesh: rep: 1, dp: 16 (over x, y, z, core).
Axes of the slice: x: 2, y: 2, z: 2, core: 2. Of those that a mesh axis runs over, the one named last changes fastest.
Arguments:
- x: bfloat16 [16, 2048, 1024], P(('rep', 'dp'))
- dy: bfloat16 [16, 2048, 1024], P(('rep', 'dp'))
- w_gate: bfloat16 [2, 1024, 4096], P(None, 'dp')
- w_up: bfloat16 [2, 1024, 4096], P(None, 'dp')
- w_down: bfloat16 [2, 4096, 1024], P(None, 'dp')
- m_w_gate: float32 [2, 1024, 4096], P(None, 'dp')
- m_w_up: float32 [2, 1024, 4096], P(None, 'dp')
- m_w_down: float32 [2, 4096, 1024], P(None, 'dp')
- v_w_gate: float32 [2, 1024, 4096], P(None, 'dp')
- v_w_up: float32 [2, 1024, 4096], P(None, 'dp')
- v_w_down: float32 [2, 4096, 1024], P(None, 'dp')
Outputs:
- output 1: bfloat16 [2, 1024, 4096], P('rep', 'dp')
- output 2: bfloat16 [2, 1024, 4096], P('rep', 'dp')
- output 3: bfloat16 [2, 4096, 1024], P('rep', 'dp')
- output 4: float32 [2, 1024, 4096], P('rep', 'dp')
- output 5: float32 [2, 1024, 4096], P('rep', 'dp')
- output 6: float32 [2, 4096, 1024], P('rep', 'dp')
- output 7: float32 [2, 1024, 4096], P('rep', 'dp')
- output 8: float32 [2, 1024, 4096], P('rep', 'dp')
- output 9: float32 [2, 4096, 1024], P('rep', 'dp')
All inputs are finite; a program needn't handle non-finite values.
Results may differ from a plain program's by a relative error of at most 0.0224.
Values are sent between devices in bfloat16 or wider.
A program may use at most 2 GiB of HBM per device.

v0:
```python
import jax
import jax.numpy as jnp
from jax import lax
from jax.sharding import PartitionSpec as P

NAMES = ("w_gate", "w_up", "w_down")


def matmul(a, w):
    return jnp.dot(a, w, preferred_element_type=jnp.float32).astype(jnp.bfloat16)


def normed(h):
    wide = h.astype(jnp.float32)
    scale = lax.rsqrt(jnp.mean(wide**2, -1, keepdims=True) + 1e-6)
    return (wide * scale).astype(jnp.bfloat16)


def layer(h, w):
    a = normed(h)
    gate = jnp.dot(a, w["w_gate"], preferred_element_type=jnp.float32)
    up = jnp.dot(a, w["w_up"], preferred_element_type=jnp.float32)
    return h + matmul((jax.nn.silu(gate) * up).astype(jnp.bfloat16), w["w_down"])


def adamw(w, m, v, g):
    m = 0.9 * m + 0.1 * g
    v = 0.95 * v + 0.05 * g * g
    step = m * lax.rsqrt(v + 1e-8) + 0.1 * w
    return (w - 0.02 * step).astype(jnp.bfloat16), m, v


def clipped(gradients, sum_of_squares, count):
    factor = jnp.minimum(1.0, 0.5 * lax.rsqrt(sum_of_squares / count + 1e-30))
    return [g * factor for g in gradients]


def solution(mesh):
    def fetched(weights, number):
        return {name: lax.all_gather(w[number], "dp", axis=0, tiled=True) for name, w in zip(NAMES, weights, strict=True)}

    def step(x, dy, *arrays):
        weights, m, v = (arrays[i : i + 3] for i in (0, 3, 6))
        layers = weights[0].shape[0]
        h, kept = x[0], []
        for number in range(layers):
            kept.append(h)
            h = layer(h, fetched(weights, number))
        by_h, mine = dy[0], [None] * layers
        for number in reversed(range(layers)):
            _, back = jax.vjp(lambda w, h: layer(h, w), fetched(weights, number), kept[number])
            by_w, by_h = back(by_h)
            mine[number] = [lax.psum_scatter(by_w[name], "dp", scatter_dimension=0, tiled=True) for name in NAMES]
        gradients = [jnp.stack([mine[number][i] for number in range(layers)]).astype(jnp.float32) for i in range(3)]
        squares = lax.psum(sum(jnp.sum(g * g) for g in gradients), "dp")
        gradients = clipped(gradients, squares, lax.psum(1, "dp") * sum(g.size for g in gradients))
        new = [adamw(w.astype(jnp.float32), m, v, g) for w, m, v, g in zip(weights, m, v, gradients, strict=True)]
        return tuple(one[which] for which in range(3) for one in new)

    states, cut = P(("rep", "dp"), None, None), P(None, "dp", None)
    return jax.shard_map(
        step,
        mesh=mesh,
        in_specs=(states, states) + (cut,) * 9,
        out_specs=(P("rep", "dp", None),) * 9,
        check_vma=False,
    )
```

profile of v0, /device:TPU:0, one launch (start us, length us, event | category | flops | bytes accessed | tf_op | source)
XLA Modules:
  0.0 1075.3 jit_solution(6584603132941788305)
XLA Ops:
  15.9 6.6 copy.20
  25.6 6.5 copy.21
  32.1 30.2 %all-gather.13.cloned.1.call-done = bf16[1,1024,4096]{2,1,0:T(8,128)(2,1)} async-done(((bf16[1,64,4096]{2,1,0:T(8,128)(2,1)}), bf16[1,1024,4096]{2,1,0:T(8,128)(2,1)}) %all-gather.13.cloned.1.call-update) | async-done | bytes 8388624 | tf_op jit(solution)/shard_map/all_gather | solution.py:40
  62.3 24.4 %fusion.35 = f32[2048,4096]{1,0:T(8,128)} fusion(bf16[1,1024,4096]{2,1,0:T(8,128)(2,1)} %all-gather.13.cloned.1.call-done, bf16[1,2048,1024]{1,2,0:T(8,128)(2,1)} %copy.20, f32[2048]{0:T(1024)S(1)} %add_rsqrt_fusion), kind=kOutput, calls=%fused_computation.53 | convolution fusion | flops 17186160640 | bytes 46145536 | tf_op jit(solution)/shard_map/dot_general | solution.py:21
  86.7 27.0 %all-gather.15.cloned.1.call-done = bf16[1,1024,4096]{2,1,0:T(8,128)(2,1)} async-done(((bf16[1,64,4096]{2,1,0:T(8,128)(2,1)}), bf16[1,1024,4096]{2,1,0:T(8,128)(2,1)}) %all-gather.15.cloned.1.call-update) | async-done | bytes 8388624 | tf_op jit(solution)/shard_map/all_gather | solution.py:40
  113.8 39.4 %multiply_convert_fusion.1 = (bf16[2048,4096]{1,0:T(8,128)(2,1)}, f32[2048,4096]{1,0:T(8,128)}) fusion(f32[2048,4096]{1,0:T(8,128)} %fusion.35, bf16[1,1024,4096]{2,1,0:T(8,128)(2,1)} %all-gather.15.cloned.1.call-done, bf16[1,2048,1024]{1,2,0:T(8,128)(2,1)} %copy.20, f32[2048]{0:T(1024)S(1)} %add_rsqrt_fusion), kind=kOutput, calls=%fused_computation.17 | convolution fusion | flops 17236492288 | bytes 96477184 | tf_op jit(solution)/shard_map/dot_general | solution.py:22
  153.2 12.1 %all-gather.17.cloned.1.call-done = bf16[1,4096,1024]{2,1,0:T(8,128)(2,1)} async-done(((bf16[1,256,1024]{2,1,0:T(8,128)(2,1)}), bf16[1,4096,1024]{2,1,0:T(8,128)(2,1)}) %all-gather.17.cloned.1.call-update) | async-done | bytes 8388624 | tf_op jit(solution)/shard_map/all_gather | solution.py:40
  165.3 24.6 %fusion.19 = (f32[2048]{0:T(1024)S(1)}, bf16[2048,1024]{0,1:T(8,128)(2,1)}) fusion(bf16[2048,4096]{1,0:T(8,128)(2,1)} %get-tuple-element.24, bf16[1,4096,1024]{2,1,0:T(8,128)(2,1)} %all-gather.17.cloned.1.call-done, bf16[1,2048,1024]{1,2,0:T(8,128)(2,1)} %copy.20), kind=kOutput, calls=%fused_computation.37 | convolution fusion | flops 17190352896 | bytes 33562624 | tf_op jit(solution)/shard_map/dot_general | solution.py:10
  190.5 26.2 %all-gather.23.cloned.1.call-done = bf16[1,1024,4096]{2,1,0:T(8,128)(2,1)} async-done(((bf16[1,64,4096]{2,1,0:T(8,128)(2,1)}), bf16[1,1024,4096]{2,1,0:T(8,128)(2,1)}) %all-gather.23.cloned.1.call-update) | async-done | bytes 8388624 | tf_op jit(solution)/shard_map/all_gather | solution.py:40
  216.6 24.5 %fusion.22 = f32[2048,4096]{1,0:T(8,128)} fusion(bf16[1,1024,4096]{2,1,0:T(8,128)(2,1)} %all-gather.23.cloned.1.call-done, bf16[2048,1024]{0,1:T(8,128)(2,1)} %get-tuple-element.27, f32[2048]{0:T(1024)S(1)} %fusion.80), kind=kOutput, calls=%fused_computation.40 | convolution fusion | flops 17186160640 | bytes 46145536 | tf_op jit(solution)/shard_map/jvp()/dot_general | solution.py:22
  241.1 26.9 %all-gather.21.cloned.1.call-done = bf16[1,4096,1024]{2,1,0:T(8,128)(2,1)} async-done(((bf16[1,256,1024]{2,1,0:T(8,128)(2,1)}), bf16[1,4096,1024]{2,1,0:T(8,128)(2,1)}) %all-gather.21.cloned.1.call-update) | async-done | bytes 8388624 | tf_op jit(solution)/shard_map/all_gather | solution.py:40
  268.0 24.5 %convolution_convert_fusion.1 = bf16[2048,4096]{1,0:T(8,128)(2,1)} fusion(bf16[1,4096,1024]{2,1,0:T(8,128)(2,1)} %all-gather.21.cloned.1.call-done, bf16[1,2048,1024]{2,1,0:T(8,128)(2,1)} %param.12), kind=kOutput, calls=%fused_computation.25 | convolution fusion | flops 17188257792 | bytes 29360128 | tf_op jit(solution)/shard_map/transpose(jvp())/dot_general | solution.py:10
  292.5 26.9 %all-gather.19.cloned.1.call-done = bf16[1,1024,4096]{2,1,0:T(8,128)(2,1)} async-done(((bf16[1,64,4096]{2,1,0:T(8,128)(2,1)}), bf16[1,1024,4096]{2,1,0:T(8,128)(2,1)}) %all-gather.19.cloned.1.call-update) | async-done | bytes 8388624 | tf_op jit(solution)/shard_map/all_gather | solution.py:40
  319.3 46.6 %fusion.2 = (bf16[2048,4096]{1,0:T(8,128)(2,1)}, f32[2048,4096]{1,0:T(8,128)}) fusion(f32[2048,4096]{1,0:T(8,128)} %fusion.22, bf16[2048,4096]{1,0:T(8,128)(2,1)} %convolution_convert_fusion.1, bf16[1,1024,4096]{2,1,0:T(8,128)(2,1)} %all-gather.19.cloned.1.call-done, bf16[2048,1024]{0,1:T(8,128)(2,1)} %get-tuple-element.27, f32[2048]{0:T(1024)S(1)} %fusion.80), kind=kOutput, calls=%fused_computation.8 | convolution fusion | flops 17286823936 | bytes 113254400 | tf_op jit(solution)/shard_map/jvp()/dot_general | solution.py:21
  365.9 27.3 %fusion.12 = bf16[2048,1024]{0,1:T(8,128)(2,1)} fusion(bf16[2048,4096]{1,0:T(8,128)(2,1)} %convolution_convert_fusion.1, bf16[1,1024,4096]{2,1,0:T(8,128)(2,1)} %all-gather.23.cloned.1.call-done, f32[2048,4096]{1,0:T(8,128)} %get-tuple-element.29), kind=kOutput, calls=%fused_computation.21 | convolution fusion | flops 17230200832 | bytes 62914560 | tf_op jit(solution)/shard_map/transpose(jvp())/dot_general | solution.py:22
  393.3 25.1 %fusion.21 = (f32[2048]{0:T(1024)S(1)}, bf16[2048,1024]{0,1:T(8,128)(2,1)S(1)}) fusion(bf16[2048,1024]{0,1:T(8,128)(2,1)S(1)} %copy-done.1, bf16[2048,1024]{0,1:T(8,128)(2,1)} %fusion.12, bf16[2048,4096]{1,0:T(8,128)(2,1)} %get-tuple-element.28, bf16[1,1024,4096]{2,1,0:T(8,128)(2,1)} %all-gather.19.cloned.1.call-done), kind=kOutput, calls=%fused_computation.39 | convolution fusion | flops 17190352896 | bytes 37756928 | tf_op jit(solution)/shard_map/transpose(jvp())/dot_general | solution.py:21
  418.5 3.1 fusion.44
  423.6 23.1 %convolution_convert_fusion.2 = bf16[4096,1024]{1,0:T(8,128)(2,1)} fusion(bf16[2048,4096]{1,0:T(8,128)(2,1)} %get-tuple-element.24, bf16[2048,1024]{0,1:T(8,128)(2,1)S(1)} %fusion.44), kind=kOutput, calls=%fused_computation.59 | convolution fusion | flops 17184063488 | bytes 29360128 | tf_op jit(solution)/shard_map/transpose(jvp())/dot_general | solution.py:10
  446.8 30.6 %fusion.40 = bf16[4096,1024]{1,0:T(8,128)(2,1)} fusion(f32[2048,4096]{1,0:T(8,128)} %fusion.22, bf16[1,2048,1024]{2,1,0:T(8,128)(2,1)} %param.12, f32[2048,4096]{1,0:T(8,128)} %get-tuple-element.29), kind=kOutput, calls=%fused_computation.56 | convolution fusion | flops 17234395136 | bytes 79691776 | tf_op jit(solution)/shard_map/transpose(jvp())/dot_general | solution.py:10
  477.4 24.9 %convolution_convert_fusion = bf16[2048,4096]{1,0:T(8,128)(2,1)} fusion(bf16[2048,1024]{0,1:T(8,128)(2,1)} %copy-done.2, bf16[1,4096,1024]{2,1,0:T(8,128)(2,1)} %all-gather.17.cloned.1.call-done), kind=kOutput, calls=%fused_computation.24 | convolution fusion | flops 17188257792 | bytes 29360128 | tf_op jit(solution)/shard_map/transpose(jvp())/dot_general | solution.py:10
  502.4 26.9 %fusion.42 = bf16[1024,4096]{1,0:T(8,128)(2,1)} fusion(bf16[2048,4096]{1,0:T(8,128)(2,1)} %convolution_convert_fusion, f32[2048,4096]{1,0:T(8,128)} %fusion.35, bf16[1,2048,1024]{1,2,0:T(8,128)(2,1)} %copy.20, f32[2048]{0:T(1024)S(1)} %copy-done.19), kind=kOutput, calls=%fused_computation.58 | convolution fusion | flops 17240686592 | bytes 62922752 | tf_op jit(solution)/shard_map/transpose(jvp())/dot_general | solution.py:22
  530.0 26.7 %fusion.41 = bf16[1024,4096]{1,0:T(8,128)(2,1)} fusion(bf16[2048,4096]{1,0:T(8,128)(2,1)} %convolution_convert_fusion.1, bf16[2048,1024]{0,1:T(8,128)(2,1)} %get-tuple-element.27, f32[2048]{0:T(1024)S(1)} %copy-done.15, f32[2048,4096]{1,0:T(8,128)} %get-tuple-element.29), kind=kOutput, calls=%fused_computation.57 | convolution fusion | flops 17240686592 | bytes 62922752 | tf_op jit(solution)/shard_map/transpose(jvp())/dot_general | solution.py:22
  556.8 37.3 %fusion.37 = bf16[1024,4096]{1,0:T(8,128)(2,1)} fusion(f32[2048,4096]{1,0:T(8,128)} %fusion.35, f32[2048,4096]{1,0:T(8,128)} %get-tuple-element.25, bf16[2048,4096]{1,0:T(8,128)(2,1)} %convolution_convert_fusion, bf16[1,2048,1024]{1,2,0:T(8,128)(2,1)} %copy.20, f32[2048]{0:T(1024)S(1)} %copy-done.19), kind=kOutput, calls=%fused_computation.55 | convolution fusion | flops 17282629632 | bytes 96477184 | tf_op jit(solution)/shard_map/transpose(jvp())/dot_general | solution.py:21
  594.1 22.9 %convolution_convert_fusion.3 = bf16[1024,4096]{1,0:T(8,128)(2,1)} fusion(bf16[2048,4096]{1,0:T(8,128)(2,1)} %get-tuple-element.28, bf16[2048,1024]{0,1:T(8,128)(2,1)} %get-tuple-element.27, f32[2048]{0:T(1024)S(1)} %copy-done.15), kind=kOutput, calls=%fused_computation.60 | convolution fusion | flops 17186160640 | bytes 29368320 | tf_op jit(solution)/shard_map/transpose(jvp())/dot_general | solution.py:21
  617.0 16.9 %reduce-scatter.17.cloned.1.call-done = bf16[256,1024]{1,0:T(8,128)(2,1)} async-done(((bf16[4096,1024]{1,0:T(8,128)(2,1)}), bf16[256,1024]{1,0:T(8,128)(2,1)}) %reduce-scatter.17.cloned.1.call-update) | async-done | bytes 524304 | tf_op jit(solution)/shard_map/reduce_scatter | solution.py:53
  636.2 93.3 %reduce-scatter.11.cloned.1.call-done = bf16[64,4096]{1,0:T(8,128)(2,1)} async-done(((bf16[1024,4096]{1,0:T(8,128)(2,1)}), bf16[64,4096]{1,0:T(8,128)(2,1)}) %reduce-scatter.11.cloned.1.call-update) | async-done | bytes 524304 | tf_op jit(solution)/shard_map/reduce_scatter | solution.py:53
  729.6 95.5 %reduce-scatter.13.cloned.1.call-done = bf16[64,4096]{1,0:T(8,128)(2,1)} async-done(((bf16[1024,4096]{1,0:T(8,128)(2,1)}), bf16[64,4096]{1,0:T(8,128)(2,1)}) %reduce-scatter.13.cloned.1.call-update) | async-done | bytes 524304 | tf_op jit(solution)/shard_map/reduce_scatter | solution.py:53
  827.4 93.4 %reduce-scatter.7.cloned.1.call-done = bf16[64,4096]{1,0:T(8,128)(2,1)} async-done(((bf16[1024,4096]{1,0:T(8,128)(2,1)}), bf16[64,4096]{1,0:T(8,128)(2,1)}) %reduce-scatter.7.cloned.1.call-update) | async-done | bytes 524304 | tf_op jit(solution)/shard_map/reduce_scatter | solution.py:53
  920.8 95.5 %reduce-scatter.9.cloned.1.call-done = bf16[64,4096]{1,0:T(8,128)(2,1)} async-done(((bf16[1024,4096]{1,0:T(8,128)(2,1)}), bf16[64,4096]{1,0:T(8,128)(2,1)}) %reduce-scatter.9.cloned.1.call-update) | async-done | bytes 524304 | tf_op jit(solution)/shard_map/reduce_scatter | solution.py:53
  1020.6 34.1 %psum.7 = f32[]{:T(128)} all-reduce(f32[]{:T(128)S(6)} %add.99), channel_id=1, replica_groups=mesh['rep'=1,'dp'=16] {'dp'}, use_global_device_ids=true, to_apply=%region_12.13 | all-reduce | flops 1 | bytes 8 | tf_op jit(solution)/shard_map/psum | solution.py:55
  1055.6 6.0 fusion.76
  1062.8 5.1 fusion.67
  (75 shorter events, 23.7 us)
Async XLA Ops:
  7.2 55.1 %all-gather.13.cloned.1.call-start = ((), (), s32[]{:S(2)}) async-start(), calls=%async_computation.12 | async-start | bytes 8912896 | tf_op jit(solution)/shard_map/all_gather | solution.py:40
  9.5 104.3 %all-gather.15.cloned.1.call-start = ((), (), s32[]{:S(2)}) async-start(), calls=%async_computation.13 | async-start | bytes 8912896 | tf_op jit(solution)/shard_map/all_gather | solution.py:40
  11.8 153.5 %all-gather.17.cloned.1.call-start = ((), (), s32[]{:S(2)}) async-start(), calls=%async_computation.14 | async-start | bytes 8912896 | tf_op jit(solution)/shard_map/all_gather | solution.py:40
  14.2 202.5 %all-gather.23.cloned.1.call-start = ((), (), s32[]{:S(2)}) async-start(), calls=%async_computation.17 | async-start | bytes 8912896 | tf_op jit(solution)/shard_map/all_gather | solution.py:40
  14.7 253.3 %all-gather.21.cloned.1.call-start = ((), (), s32[]{:S(2)}) async-start(), calls=%async_computation.16 | async-start | bytes 8912896 | tf_op jit(solution)/shard_map/all_gather | solution.py:40
  15.3 304.0 %all-gather.19.cloned.1.call-start = ((), (), s32[]{:S(2)}) async-start(), calls=%async_computation.15 | async-start | bytes 8912896 | tf_op jit(solution)/shard_map/all_gather | solution.py:40
  15.9 601.1 %reduce-scatter.15.cloned.1.call-start = ((), (), s32[]{:S(2)}) async-start(), calls=%async_computation.10 | async-start | bytes 8912896 | tf_op jit(solution)/shard_map/reduce_scatter | solution.py:53
  25.6 88.2 %copy-start.18 = (f32[2048]{0:T(1024)}, f32[2048]{0:T(1024)S(1)}, u32[]{:S(2)}) copy-start(f32[2048]{0:T(1024)S(1)} %add_rsqrt_fusion) | copy-start | bytes 24580
  189.9 0.6 copy-start.16
  190.5 228.0 %copy-start.14 = (f32[2048]{0:T(1024)}, f32[2048]{0:T(1024)S(1)}, u32[]{:S(2)}) copy-start(f32[2048]{0:T(1024)S(1)} %fusion.80) | copy-start | bytes 24580
  365.9 27.3 %copy-start.1 = (bf16[2048,1024]{0,1:T(8,128)(2,1)S(1)}, bf16[2048,1024]{0,1:T(8,128)(2,1)}, u32[]{:S(2)}) copy-start(bf16[2048,1024]{0,1:T(8,128)(2,1)} %get-tuple-element.27) | copy-start | bytes 12582916
  393.3 25.1 %copy-start.17 = (f32[2048]{0:T(1024)S(1)}, f32[2048]{0:T(1024)}, u32[]{:S(2)}) copy-start(f32[2048]{0:T(1024)} %copy-done.16) | copy-start | bytes 24580
  393.3 25.2 %copy-start = (bf16[1,2048,1024]{1,2,0:T(8,128)(2,1)S(1)}, bf16[1,2048,1024]{1,2,0:T(8,128)(2,1)}, u32[]{:S(2)}) copy-start(bf16[1,2048,1024]{1,2,0:T(8,128)(2,1)} %copy.21) | copy-start | bytes 12582916
  421.6 2.0 copy-start.2
  446.8 187.2 %reduce-scatter.17.cloned.1.call-start = ((), (), s32[]{:S(2)}) async-start(), calls=%async_computation.11 | async-start | bytes 8912896 | tf_op jit(solution)/shard_map/reduce_scatter | solution.py:53
  477.4 25.0 %copy-start.19 = (f32[2048]{0:T(1024)S(1)}, f32[2048]{0:T(1024)}, u32[]{:S(2)}) copy-start(f32[2048]{0:T(1024)} %copy-done.18) | copy-start | bytes 24580
  477.4 252.2 %reduce-scatter.11.cloned.1.call-start = ((), (), s32[]{:S(2)}) async-start(), calls=%async_computation.8 | async-start | bytes 8912896 | tf_op jit(solution)/shard_map/reduce_scatter | solution.py:53
  529.3 0.7 copy-start.15
  529.3 295.8 %reduce-scatter.13.cloned.1.call-start = ((), (), s32[]{:S(2)}) async-start(), calls=%async_computation.9 | async-start | bytes 8912896 | tf_op jit(solution)/shard_map/reduce_scatter | solution.py:53
  556.7 364.1 %reduce-scatter.7.cloned.1.call-start = ((), (), s32[]{:S(2)}) async-start(), calls=%async_computation.6 | async-start | bytes 8912896 | tf_op jit(solution)/shard_map/reduce_scatter | solution.py:53
  594.0 422.3 %reduce-scatter.9.cloned.1.call-start = ((), (), s32[]{:S(2)}) async-start(), calls=%async_computation.7 | async-start | bytes 8912896 | tf_op jit(solution)/shard_map/reduce_scatter | solution.py:53
  617.0 438.5 %copy-start.3 = (bf16[2,256,1024]{2,1,0:T(8,128)(2,1)S(1)}, bf16[2,256,1024]{2,1,0:T(8,128)(2,1)}, u32[]{:S(2)}) copy-start(bf16[2,256,1024]{2,1,0:T(8,128)(2,1)} %param.15) | copy-start | bytes 3145732
  617.0 444.5 %copy-start.4 = (bf16[2,64,4096]{2,1,0:T(8,128)(2,1)S(1)}, bf16[2,64,4096]{2,1,0:T(8,128)(2,1)}, u32[]{:S(2)}) copy-start(bf16[2,64,4096]{2,1,0:T(8,128)(2,1)} %param.13) | copy-start | bytes 3145732
  617.0 444.5 %copy-start.5 = (bf16[2,64,4096]{2,1,0:T(8,128)(2,1)S(1)}, bf16[2,64,4096]{2,1,0:T(8,128)(2,1)}, u32[]{:S(2)}) copy-start(bf16[2,64,4096]{2,1,0:T(8,128)(2,1)} %param.14) | copy-start | bytes 3145732
  1055.5 6.1 copy-start.6
  1055.5 6.0 copy-start.7
  1055.5 6.0 copy-start.8
  1055.5 6.5 copy-start.9
  1055.5 6.9 copy-start.10
  1055.5 7.0 copy-start.11
  1055.5 7.2 copy-start.12
  1055.5 7.3 copy-start.13
Sparse Core Ops, SparseCore 0:
  10.8 51.4 all-gather.12
  65.1 48.6 all-gather.14
  116.6 48.6 all-gather.16
  168.0 48.6 all-gather.22
  219.3 48.6 all-gather.20
  270.7 48.6 all-gather.18
  446.9 91.3 reduce-scatter.14
  540.5 93.3 reduce-scatter.16
  636.2 93.3 reduce-scatter.10
  731.7 93.3 reduce-scatter.12
  827.4 93.3 reduce-scatter.6
  922.9 93.3 reduce-scatter.8
where the time goes:
time: 1080 us
  waiting for transfers between devices  546 us (51%)
  matrix products  429 us (40%)
  blocking collectives  34.1 us (3%)
  local copies, waits for them, and re-layouts  24.4 us (2%)
  other arithmetic  24.3 us (2%)
  between operations  17.6 us (2%)
    reduce_scatter x6, waiting for transfers between devices, step(): lax.psum_scatter(by_w[name], 'dp', scatter_dimension=0, tiled=True)  395 us
    dot_general x5, matrix products, layer(): gate = jnp.dot(a, w['w_gate'], preferred_element_type=jnp.float32)  156 us
    all_gather x6, waiting for transfers between devices, fetched(): lax.all_gather(w[number], 'dp', axis=0, tiled=True)  149 us
    dot_general x5, matrix products, layer(): up = jnp.dot(a, w['w_up'], preferred_element_type=jnp.float32)  145 us
    dot_general x5, matrix products, matmul(): jnp.dot(a, w, preferred_element_type=jnp.float32).astype(jnp.bfloat16)  128 us
    psum x1, blocking collectives, step(): squares = lax.psum(sum((jnp.sum(g * g) for g in gradients)), 'dp')  34.1 us
  transfers between devices with their start and end apart: 12, of which 11 were waited for; matrix products, arithmetic and copies ran while one was open for 31% of the time, Pallas kernels for 0%

commit v1 on v0

v1 whole, which is shorter than its diff:
```python
import functools

import jax
import jax.numpy as jnp
from jax import lax
from jax.experimental import pallas as pl
from jax.experimental.pallas import tpu as pltpu
from jax.sharding import PartitionSpec as P

F32, BF16 = jnp.float32, jnp.bfloat16
NAMES = ("w_gate", "w_up", "w_down")
BITS = (8, 4, 2)
VMEM_LIMIT = 66_000_000


def normed(h):
    wide = h.astype(F32)
    scale = lax.rsqrt(jnp.mean(wide**2, -1, keepdims=True) + 1e-6)
    return (wide * scale).astype(BF16)


def adamw(w, m, v, g):
    m = 0.9 * m + 0.1 * g
    v = 0.95 * v + 0.05 * g * g
    step = m * lax.rsqrt(v + 1e-8) + 0.1 * w
    return (w - 0.02 * step).astype(BF16), m, v


def clipped(gradients, sum_of_squares, count):
    factor = jnp.minimum(1.0, 0.5 * lax.rsqrt(sum_of_squares / count + 1e-30))
    return [g * factor for g in gradients]


def thirds(columns):
    tiles, start, out = columns // 128, 0, []
    for k in range(3):
        size = 128 * (tiles // 3 + (k < tiles % 3))
        out.append((start, size))
        start += size
    return out


class Place:
    def __init__(self):
        me = lax.axis_index("dp")
        self.core = me % 2
        self.at = (me // 8, (me // 4) % 2, (me // 2) % 2)
        self.near = tuple(me + bit * (1 - 2 * v) for bit, v in zip(BITS, self.at))
        self.twin = me + 1 - 2 * self.core

    def greet(self):
        barrier = pltpu.get_barrier_semaphore()
        for other in (*self.near, self.twin):
            pl.semaphore_signal(barrier, inc=1, device_id={"dp": other}, device_id_type=pl.DeviceIdType.MESH)
        pl.semaphore_wait(barrier, 4)


def remote(src, dst, send, recv, device):
    return pltpu.make_async_remote_copy(
        src_ref=src, dst_ref=dst, send_sem=send, recv_sem=recv, device_id={"dp": device}, device_id_type=pl.DeviceIdType.MESH
    )


class Gather:
    def __init__(self, place, own, full, send, recv, here):
        self.place, self.own, self.full, self.send, self.recv, self.here = place, own, full, send, recv, here
        self.cuts = thirds(own.shape[-1])

    def local(self):
        x, y, z = self.place.at
        return pltpu.make_async_copy(self.own, self.full.at[x, y, z, self.place.core], self.here)

    def copy(self, stage, k):
        order = [(k + j) % 3 for j in range(3)]
        at = list(self.place.at)
        for d in order[:stage]:
            at[d] = slice(None)
        columns = pl.ds(*self.cuts[k])
        region = self.full.at[(*at, self.place.core, slice(None), columns)]
        src = region if stage else self.own.at[:, columns]
        n = 3 * stage + k
        return remote(src, region, self.send.at[n], self.recv.at[n], self.place.near[order[stage]])

    def across(self):
        region = self.full.at[:, :, :, self.place.core]
        return remote(region, region, self.send.at[9], self.recv.at[9], self.place.twin)

    def act(self, j):
        if j == 0:
            self.local().start()
            for k in range(3):
                self.copy(0, k).start()
        elif j in (1, 2):
            if j == 1:
                self.local().wait()
            for k in range(3):
                self.copy(j - 1, k).wait_recv()
                self.copy(j, k).start()
        elif j == 3:
            for k in range(3):
                self.copy(2, k).wait_recv()
            self.across().start()
        else:
            self.across().wait_recv()
            for stage in range(3):
                for k in range(3):
                    self.copy(stage, k).wait_send()
            self.across().wait_send()


def gather_scratch():
    return [pltpu.SemaphoreType.DMA((10,)), pltpu.SemaphoreType.DMA((10,)), pltpu.SemaphoreType.DMA]


class Scatter:
    def __init__(self, place, partial, out, total, first, landed, send, recv, here):
        self.place, self.partial, self.out, self.total, self.first = place, partial, out, total, first
        self.landed, self.send, self.recv, self.here = landed, send, recv, here
        self.rows, self.columns = partial.shape[-2:]
        self.cuts = thirds(self.columns)
        self.strip = 16

    def load(self):
        return pltpu.make_async_copy(self.partial.at[:, :, :, self.place.core], self.total, self.here)

    def across(self):
        return remote(self.partial.at[:, :, :, 1 - self.place.core], self.first, self.send.at[9], self.recv.at[9], self.place.twin)

    def where(self, stage, k, keep):
        order = [(k + j) % 3 for j in range(3)]
        at = [slice(None)] * 3
        for d in order[:stage]:
            at[d] = self.place.at[d]
        d = order[stage]
        at[d] = self.place.at[d] if keep else 1 - self.place.at[d]
        return at, d

    def copy(self, stage, k):
        at, d = self.where(stage, k, False)
        n = 3 * stage + k
        return remote(
            self.total.at[(*at, slice(None), pl.ds(*self.cuts[k]))], self.landed[n], self.send.at[n], self.recv.at[n], self.place.near[d]
        )

    def add_first(self):
        @pl.loop(0, 8)
        def _(block):
            at = (block // 4, (block // 2) % 2, block % 2)

            @pl.loop(0, self.rows // self.strip)
            def _(strip):
                to = (*at, pl.ds(strip * self.strip, self.strip), slice(None))
                self.total[to] = (self.total[to].astype(F32) + self.first[to].astype(F32)).astype(BF16)

    def add(self, stage, k):
        at, _ = self.where(stage, k, True)
        landed, free = self.landed[3 * stage + k], [d for d in range(3) if isinstance(at[d], slice)]
        columns = pl.ds(*self.cuts[k])
        for number in range(2 ** len(free)):
            bits = [(number >> b) & 1 for b in reversed(range(len(free)))]
            spot = list(at)
            for d, bit in zip(free, bits):
                spot[d] = bit

            @pl.loop(0, self.rows // self.strip)
            def _(strip, spot=spot, bits=bits):
                rows = pl.ds(strip * self.strip, self.strip)
                to = (*spot, rows, columns)
                value = (self.total[to].astype(F32) + landed[(*bits, rows, slice(None))].astype(F32)).astype(BF16)
                if stage < 2:
                    self.total[to] = value
                else:
                    self.out[rows, columns] = value

    def act(self, j):
        if j == 0:
            self.across().start()
            self.load().start()
        elif j == 1:
            self.load().wait()
            self.across().wait_recv()
            self.add_first()
            for k in range(3):
                self.copy(0, k).start()
        elif j in (2, 3):
            for k in range(3):
                self.copy(j - 2, k).wait_recv()
                self.add(j - 2, k)
                self.copy(j - 1, k).start()
        else:
            for k in range(3):
                self.copy(2, k).wait_recv()
                self.add(2, k)
            for stage in range(3):
                for k in range(3):
                    self.copy(stage, k).wait_send()
            self.across().wait_send()


def scatter_scratch(rows, columns):
    landed = [pltpu.VMEM((2,) * (2 - stage) + (rows, size), BF16) for stage in range(3) for _, size in thirds(columns)]
    whole = pltpu.VMEM((2, 2, 2, rows, columns), BF16)
    return [whole, whole, *landed, pltpu.SemaphoreType.DMA((10,)), pltpu.SemaphoreType.DMA((10,)), pltpu.SemaphoreType.DMA]


ANY = pl.BlockSpec(memory_space=pl.ANY)


def once(shape):
    return pl.BlockSpec(shape, lambda i: (0,) * len(shape), pipeline_mode=pl.Buffered(1))


def fused(name, cid, steps, body, ins, in_specs, outs, out_specs, scratch, gathers=(), scatters=()):
    n_in, n_out = len(ins), len(outs)
    ng, ns = len(gathers), len(scatters)
    sizes = [w.shape[1:] for w, _, _ in gathers]
    in_specs, ins, outs, out_specs = list(in_specs), list(ins), list(outs), list(out_specs)
    scratch = list(scratch)
    n_scratch = len(scratch)
    for (w, layer, _), (r, c) in zip(gathers, sizes):
        ins.append(w)
        in_specs.append(pl.BlockSpec((1, r, c), lambda i, layer=layer: (layer, 0, 0), pipeline_mode=pl.Buffered(1)))
        outs.append(jax.ShapeDtypeStruct((2, 2, 2, 2, r, c), BF16))
        out_specs.append(ANY)
        scratch += gather_scratch()
    for d, _ in scatters:
        r, c = d.shape[-2:]
        ins.append(d)
        in_specs.append(ANY)
        outs.append(jax.ShapeDtypeStruct((r, c), BF16))
        out_specs.append(pl.BlockSpec((r, c), lambda i: (0, 0), pipeline_mode=pl.Buffered(1)))
        scratch += scatter_scratch(r, c)

    def kernel(*refs):
        refs = list(refs)
        i_refs, refs = refs[: n_in + ng + ns], refs[n_in + ng + ns :]
        o_refs, refs = refs[: n_out + ng + ns], refs[n_out + ng + ns :]
        own_scratch, refs = refs[:n_scratch], refs[n_scratch:]
        place = Place()
        exchanges = []
        for g in range(ng):
            exchanges.append((Gather(place, i_refs[n_in + g].at[0], o_refs[n_out + g], *refs[:3]), gathers[g][2]))
            refs = refs[3:]
        for s in range(ns):
            part, out = i_refs[n_in + ng + s], o_refs[n_out + ng + s]
            exchanges.append((Scatter(place, part, out, refs[0], refs[1], refs[2:11], *refs[11:14]), scatters[s][1]))
            refs = refs[14:]
        step = pl.program_id(0)

        def acts(at):
            for j in range(5):
                for exchange, when in exchanges:
                    if when[j] == at:
                        exchange.act(j)

        for at in sorted({w for _, when in exchanges for w in when if w < steps} | {0}):

            @pl.when(step == at)
            def _(at=at):
                if at == 0:
                    place.greet()
                acts(at)

        body(step, *i_refs[:n_in], *o_refs[:n_out], *own_scratch)

        @pl.when(step == steps - 1)
        def _():
            acts(steps)

    return pl.pallas_call(
        kernel,
        grid=(steps,),
        in_specs=in_specs,
        out_specs=out_specs,
        out_shape=outs,
        scratch_shapes=scratch,
        name=name,
        compiler_params=pltpu.CompilerParams(
            dimension_semantics=("arbitrary",), collective_id=cid, has_side_effects=True, vmem_limit_bytes=VMEM_LIMIT
        ),
    )(*ins)


def dot(a, b, contract=(1, 0)):
    return lax.dot_general(a, b, (((contract[0],), (contract[1],)), ((), ())), preferred_element_type=F32)


CHUNK = 512


def chunks(tokens, do):
    @pl.loop(0, tokens // CHUNK)
    def _(m):
        do(pl.ds(pl.multiple_of(m * CHUNK, CHUNK), CHUNK))


def forward_body(last, step, a, wg, wu, wd, gate, up, out, total):
    @pl.when(step == 0)
    def _():
        total[...] = jnp.zeros_like(total)

    def do(rows):
        g, u = dot(a[rows, :], wg[...]), dot(a[rows, :], wu[...])
        gate[rows, :], up[rows, :] = g, u
        hidden = (g * jax.nn.sigmoid(g) * u).astype(BF16)
        total[rows, :] += dot(hidden, wd[...])

    chunks(a.shape[0], do)

    @pl.when(step == last)
    def _():
        chunks(a.shape[0], lambda rows: out.__setitem__((rows, slice(None)), total[rows, :].astype(BF16)))


def forward_last_body(step, a, wg, wu, dy, gate, up, dwd, hidden):
    def do(rows):
        g, u = dot(a[rows, :], wg[...]), dot(a[rows, :], wu[...])
        gate[rows, :], up[rows, :] = g, u
        hidden[rows, :] = (g * jax.nn.sigmoid(g) * u).astype(BF16)

    chunks(a.shape[0], do)
    dwd[...] = dot(hidden[...], dy[...], (0, 0)).astype(BF16)


def through_gate(dy, wd, gate, up, dgate, dup, hidden, rows):
    by_hidden = dot(dy[rows, :], wd[...], (1, 1)).astype(BF16).astype(F32)
    g, u = gate[rows, :], up[rows, :]
    s = jax.nn.sigmoid(g)
    silu = g * s
    dup[rows, :] = (by_hidden * silu).astype(BF16)
    dgate[rows, :] = (by_hidden * u * (s + silu * (1.0 - s))).astype(BF16)
    if hidden is not None:
        hidden[rows, :] = (silu * u).astype(BF16)


def turn(a, at):
    for m in range(a.shape[0] // 256):
        at[:, m * 256 : (m + 1) * 256] = a[m * 256 : (m + 1) * 256, :].T


def back_last_body(step, dy, wd, gate, up, a, dgate, dup, dwg, dwu, at):
    @pl.when(step == 0)
    def _():
        turn(a, at)

    chunks(a.shape[0], lambda rows: through_gate(dy, wd, gate, up, dgate, dup, None, rows))
    dwg[...] = dot(at[...], dgate[...]).astype(BF16)
    dwu[...] = dot(at[...], dup[...]).astype(BF16)


def by_input_body(last, step, dgate, dup, wg, wu, out, total):
    @pl.when(step == 0)
    def _():
        total[...] = jnp.zeros_like(total)

    def do(rows):
        total[rows, :] += dot(dgate[rows, :], wg[...], (1, 1)) + dot(dup[rows, :], wu[...], (1, 1))

    chunks(dgate.shape[0], do)

    @pl.when(step == last)
    def _():
        chunks(dgate.shape[0], lambda rows: out.__setitem__((rows, slice(None)), total[rows, :].astype(BF16)))


def back_first_body(step, dy, wd, gate, up, dgate, dup, dwd, hidden):
    chunks(dy.shape[0], lambda rows: through_gate(dy, wd, gate, up, dgate, dup, hidden, rows))
    dwd[...] = dot(hidden[...], dy[...], (0, 0)).astype(BF16)


def weights_body(step, a, dgate, dup, dwg, dwu, at):
    @pl.when(step == 0)
    def _():
        turn(a, at)

    dwg[...] = dot(at[...], dgate[...]).astype(BF16)
    dwu[...] = dot(at[...], dup[...]).astype(BF16)


def nothing(step):
    pass


def solution(mesh):
    def step(x, dy, *arrays):
        weights, m, v = (arrays[i : i + 3] for i in (0, 3, 6))
        w_gate, w_up, w_down = weights
        x, dy = x[0], dy[0]
        tokens, d = x.shape
        ff = w_gate.shape[-1]
        tile = 256
        n = ff // tile

        def of(shape, dtype=BF16):
            return jax.ShapeDtypeStruct(shape, dtype)

        def columns(rows, width=tile):
            return pl.BlockSpec((rows, width), lambda i: (0, i))

        def rows_of(width, height=tile):
            return pl.BlockSpec((height, width), lambda i: (i, 0))

        def flat(full):
            return full.reshape(-1, full.shape[-1])

        def blocks(dw):
            return dw.reshape(2, 2, 2, 2, dw.shape[0] // 16, dw.shape[1])

        here = once((tokens, d))
        zero = (0,) * 5
        g0, u0, d0 = fused("fetch", 1, 1, nothing, [], [], [], [], [], gathers=[(w, 0, (0, 0, 0, 1, 1)) for w in weights])
        g0, u0, d0 = map(flat, (g0, u0, d0))
        a0 = normed(x)
        states = [of((tokens, ff), F32)] * 2
        gate0, up0, out0, g1, u1 = fused(
            "forward0", 2, n, functools.partial(forward_body, n - 1),
            [a0, g0, u0, d0], [here, columns(d), columns(d), rows_of(d)],
            [*states, of((tokens, d))], [columns(tokens), columns(tokens), here],
            [pltpu.VMEM((tokens, d), F32)],
            gathers=[(w_gate, 1, (0, 2, 5, 12, 15)), (w_up, 1, (0, 3, 7, n, n))],
        )
        g1, u1 = map(flat, (g1, u1))
        h1 = x + out0
        a1 = normed(h1)
        gate1, up1, dwd1, d1 = fused(
            "forward1", 3, n, forward_last_body,
            [a1, g1, u1, dy], [here, columns(d), columns(d), here],
            [*states, of((ff, d))], [columns(tokens), columns(tokens), rows_of(d)],
            [pltpu.VMEM((tokens, tile), BF16)],
            gathers=[(w_down, 1, (0, 2, 5, 10, 13))],
        )
        d1 = flat(d1)
        halves = [of((tokens, ff))] * 2
        dgate1, dup1, dwg1, dwu1, sd1 = fused(
            "back1", 4, n, back_last_body,
            [dy, d1, gate1, up1, a1], [here, rows_of(d), columns(tokens), columns(tokens), here],
            [*halves, of((d, ff)), of((d, ff))], [columns(tokens), columns(tokens), columns(d), columns(d)],
            [pltpu.VMEM((d, tokens), BF16)],
            scatters=[(blocks(dwd1), (0, 3, 8, 11, 13))],
        )
        wide = 512
        by_a1, sg1 = fused(
            "by_input1", 5, ff // wide, functools.partial(by_input_body, ff // wide - 1),
            [dgate1, dup1, g1, u1], [columns(tokens, wide), columns(tokens, wide), columns(d, wide), columns(d, wide)],
            [of((tokens, d))], [here],
            [pltpu.VMEM((tokens, d), F32)],
            scatters=[(blocks(dwg1), (0, 2, 6, 8, 8))],
        )
        (by_norm,) = jax.vjp(normed, h1)[1](by_a1)
        by_h = dy + by_norm
        dgate0, dup0, dwd0, su1 = fused(
            "back0", 6, n, back_first_body,
            [by_h, d0, gate0, up0], [here, rows_of(d), columns(tokens), columns(tokens)],
            [*halves, of((ff, d))], [columns(tokens), columns(tokens), rows_of(d)],
            [pltpu.VMEM((tokens, tile), BF16)],
            scatters=[(blocks(dwu1), (0, 4, 11, 15, n))],
        )
        dwg0, dwu0, sd0 = fused(
            "weights0", 7, n, weights_body,
            [a0, dgate0, dup0], [here, columns(tokens), columns(tokens)],
            [of((d, ff)), of((d, ff))], [columns(d), columns(d)],
            [pltpu.VMEM((d, tokens), BF16)],
            scatters=[(blocks(dwd0), (0, 4, 11, 15, n))],
        )
        sg0, su0 = fused("finish", 8, 1, nothing, [], [], [], [], [], scatters=[(blocks(dw), (0, 0, 1, 1, 1)) for dw in (dwg0, dwu0)])
        gradients = [jnp.stack(pair).astype(F32) for pair in ((sg0, sg1), (su0, su1), (sd0, sd1))]
        squares = lax.psum(sum(jnp.sum(g * g) for g in gradients), "dp")
        gradients = clipped(gradients, squares, lax.psum(1, "dp") * sum(g.size for g in gradients))
        new = [adamw(w.astype(F32), m, v, g) for w, m, v, g in zip(weights, m, v, gradients, strict=True)]
        return tuple(one[which] for which in range(3) for one in new)

    states, cut = P(("rep", "dp"), None, None), P(None, "dp", None)
    return jax.shard_map(
        step,
        mesh=mesh,
        in_specs=(states, states) + (cut,) * 9,
        out_specs=(P("rep", "dp", None),) * 9,
        check_vma=False,
    )
```

time: 1080 us -> 666 us (0.62)
  Pallas kernels: 0 us -> 585 us
  waiting for transfers between devices: 546 us -> 0 us
  matrix products: 429 us -> 0 us
  local copies, waits for them, and re-layouts: 24.4 us -> 4.9 us
  other arithmetic: 24.3 us -> 40.4 us
  between operations: 17.6 us -> 3.55 us
    pallas_call x0 -> x8, Pallas kernels: none -> 585 us  [fused(): pl.pallas_call(kernel, grid=(steps,), in_specs=in_specs, out_specs=out_sp...]
    dot_general x15 -> x0, matrix products: 429 us -> none  [the longest x5 156 us: layer(): gate = jnp.dot(a, w['w_gate'], preferred_element_type=jnp.float32)]
    reduce_scatter x6 -> x0, waiting for transfers between devices: 395 us -> none  [step(): lax.psum_scatter(by_w[name], 'dp', scatter_dimension=0, tiled=True)]
    all_gather x6 -> x0, waiting for transfers between devices: 149 us -> none  [fetched(): lax.all_gather(w[number], 'dp', axis=0, tiled=True)]
    unnamed x42 -> x32, local copies, waits for them, and re-layouts: 17.7 us -> 4.9 us
  transfers between devices with their start and end apart: 12 -> 0, of which waited for: 11 -> 0; matrix products, arithmetic and copies ran while one was open for 31% -> 0% of each run, Pallas kernels for 0% -> 0%
where the time goes in v1:
time: 666 us
  Pallas kernels  585 us (88%)
  other arithmetic  40.4 us (6%)
  blocking collectives  31.9 us (5%)
    pallas_call x8, Pallas kernels, fused(): pl.pallas_call(kernel, grid=(steps,), in_specs=in_specs, out_specs=out_sp...  585 us
    psum x1, blocking collectives, step(): squares = lax.psum(sum((jnp.sum(g * g) for g in gradients)), 'dp')  31.9 us

profile of v1, /device:TPU:0, one launch (start us, length us, event | category | flops | bytes accessed | tf_op | source)
XLA Modules:
  0.0 666.0 jit_solution(13648952808323282713)
XLA Ops:
  0.6 0.0 copy-start.3
  0.7 3.2 fusion
  3.9 0.2 copy-done.3
  4.1 2.7 fusion.1.refs_0_
  6.8 95.4 %fetch.1 = (bf16[2,2,2,2,64,4096]{5,4,3,2,1,0:T(8,128)(2,1)}, bf16[2,2,2,2,64,4096]{5,4,3,2,1,0:T(8,128)(2,1)}, bf16[2,2,2,2,256,1024]{5,4,3,2,1,0:T(8,128)(2,1)}) custom-call(bf16[2,64,4096]{2,1,0:T(8,128)(2,1)} %refs_4_.2, bf16[2,64,4096]{2,1,0:T(8,128)(2,1)} %refs_5_.1, bf16[2,256,1024]{2,1,0:T(8,128)(2,1)} %refs_4_.3), custom_call_target="tpu_custom_call" | custom-call | tf_op jit(solution)/shard_map/fetch/pallas_call | solution.py:270
  102.2 83.1 %forward0.1 = (f32[2048,4096]{1,0:T(8,128)}, f32[2048,4096]{1,0:T(8,128)}, bf16[2048,1024]{1,0:T(8,128)(2,1)}, bf16[2,2,2,2,64,4096]{5,4,3,2,1,0:T(8,128)(2,1)}, bf16[2,2,2,2,64,4096]{5,4,3,2,1,0:T(8,128)(2,1)}) custom-call(bf16[2048,1024]{1,0:T(8,128)(2,1)} %fusion.1.refs_0_, bf16[1024,4096]{1,0:T(8,128)(2,1)} %bitcast.37, bf16[1024,4096]{1,0:T(8,128)(2,1)} %bitcast.38, ...), custom_call_target="tpu_custom_call" | custom-call | tf_op jit(solution)/shard_map/forward0/pallas_call | solution.py:270
  185.4 5.0 fusion.4
  190.4 1.9 copy-done
  192.4 2.7 fusion.5.refs_0_.refs_4_
  195.1 74.9 %forward1.1 = (f32[2048,4096]{1,0:T(8,128)}, f32[2048,4096]{1,0:T(8,128)}, bf16[4096,1024]{1,0:T(8,128)(2,1)}, bf16[2,2,2,2,256,1024]{5,4,3,2,1,0:T(8,128)(2,1)}) custom-call(bf16[2048,1024]{1,0:T(8,128)(2,1)} %fusion.5.refs_0_.refs_4_, bf16[1024,4096]{1,0:T(8,128)(2,1)} %bitcast.27, bf16[1024,4096]{1,0:T(8,128)(2,1)} %bitcast.29, ...), custom_call_target="tpu_custom_call" | custom-call | tf_op jit(solution)/shard_map/forward1/pallas_call | solution.py:270
  270.0 87.0 %back1.1 = (bf16[2048,4096]{1,0:T(8,128)(2,1)}, bf16[2048,4096]{1,0:T(8,128)(2,1)}, bf16[1024,4096]{1,0:T(8,128)(2,1)}, bf16[1024,4096]{1,0:T(8,128)(2,1)}, bf16[256,1024]{1,0:T(8,128)(2,1)}) custom-call(bf16[2048,1024]{1,0:T(8,128)(2,1)} %bitcast.26, bf16[4096,1024]{1,0:T(8,128)(2,1)} %bitcast.41, f32[2048,4096]{1,0:T(8,128)} %get-tuple-element.44.refs_2_, ...), custom_call_target="tpu_custom_call" | custom-call | tf_op jit(solution)/shard_map/back1/pallas_call | solution.py:270
  357.0 56.4 %by_input1.1 = (bf16[2048,1024]{1,0:T(8,128)(2,1)}, bf16[64,4096]{1,0:T(8,128)(2,1)}) custom-call(bf16[2048,4096]{1,0:T(8,128)(2,1)} %get-tuple-element.47.refs_0_, bf16[2048,4096]{1,0:T(8,128)(2,1)} %get-tuple-element.48.refs_1_, bf16[1024,4096]{1,0:T(8,128)(2,1)} %bitcast.28, bf16[1024,4096]{1,0:T(8,128)(2,1)} %bitcast.30, ...), custom_call_target="tpu_custom_call" | custom-call | tf_op jit(solution)/shard_map/by_input1/pallas_call | solution.py:270
  413.5 0.0 copy-start.2
  413.5 4.8 fusion.6
  418.3 1.1 copy-done.2
  419.4 5.2 fusion.7.refs_0_
  424.6 69.4 %back0.1 = (bf16[2048,4096]{1,0:T(8,128)(2,1)}, bf16[2048,4096]{1,0:T(8,128)(2,1)}, bf16[4096,1024]{1,0:T(8,128)(2,1)}, bf16[64,4096]{1,0:T(8,128)(2,1)}) custom-call(bf16[2048,1024]{1,0:T(8,128)(2,1)} %fusion.7.refs_0_, bf16[4096,1024]{1,0:T(8,128)(2,1)} %bitcast.32, f32[2048,4096]{1,0:T(8,128)} %get-tuple-element.51.refs_2_, ...), custom_call_target="tpu_custom_call" | custom-call | tf_op jit(solution)/shard_map/back0/pallas_call | solution.py:270
  494.1 53.6 %weights0.1 = (bf16[1024,4096]{1,0:T(8,128)(2,1)}, bf16[1024,4096]{1,0:T(8,128)(2,1)}, bf16[256,1024]{1,0:T(8,128)(2,1)}) custom-call(bf16[2048,1024]{1,0:T(8,128)(2,1)} %fusion.1.refs_0_, bf16[2048,4096]{1,0:T(8,128)(2,1)} %get-tuple-element.54.refs_1_, bf16[2048,4096]{1,0:T(8,128)(2,1)} %get-tuple-element.55.refs_2_, bf16[2,2,2,2,256,1024]{5,4,3,2,1,0:T(8,128)(2,1)} %bitcast.36), custom_call_target="tpu_custom_call" | custom-call | tf_op jit(solution)/shard_map/weights0/pallas_call | solution.py:270
  547.7 2.2 fusion.19
  549.8 65.3 %finish.1 = (bf16[64,4096]{1,0:T(8,128)(2,1)}, bf16[64,4096]{1,0:T(8,128)(2,1)}) custom-call(bf16[2,2,2,2,64,4096]{5,4,3,2,1,0:T(8,128)(2,1)} %bitcast.34, bf16[2,2,2,2,64,4096]{5,4,3,2,1,0:T(8,128)(2,1)} %bitcast.35), custom_call_target="tpu_custom_call" | custom-call | tf_op jit(solution)/shard_map/finish/pallas_call | solution.py:270
  615.2 0.0 copy-start.4
  615.2 2.8 fusion.17
  619.9 31.9 %psum.7 = f32[]{:T(128)} all-reduce(f32[]{:T(128)S(6)} %add.80), channel_id=1, replica_groups=mesh['rep'=1,'dp'=16] {'dp'}, use_global_device_ids=true, to_apply=%region_6.0 | all-reduce | flops 1 | bytes 8 | tf_op jit(solution)/shard_map/psum | solution.py:467
  652.5 0.0 copy-start.5
  652.5 0.0 copy-start.12
  652.6 5.7 fusion.25
  658.3 0.0 copy-start.6
  658.3 0.0 copy-start.14
  658.3 3.1 fusion.16
  661.5 0.8 copy-done.14
  662.3 0.7 copy-done.15
  663.0 3.0 fusion.22
  (23 shorter events, 0.1 us)
Async XLA Ops:
  0.6 3.5 copy-start.3
  190.4 2.0 copy-start
  413.5 4.8 copy-start.1
  413.5 5.9 copy-start.2
  494.1 53.6 %copy-start.7 = (bf16[256,1024]{1,0:T(8,128)(2,1)S(1)}, bf16[256,1024]{1,0:T(8,128)(2,1)}, u32[]{:S(2)}) copy-start(bf16[256,1024]{1,0:T(8,128)(2,1)} %get-tuple-element.64) | copy-start | bytes 1572868
  615.2 37.3 %copy-start.4 = (bf16[2,256,1024]{2,1,0:T(8,128)(2,1)S(1)}, bf16[2,256,1024]{2,1,0:T(8,128)(2,1)}, u32[]{:S(2)}) copy-start(bf16[2,256,1024]{2,1,0:T(8,128)(2,1)} %refs_4_.3) | copy-start | bytes 3145732
  652.5 5.7 copy-start.5
  652.5 5.7 copy-start.8
  652.5 5.7 copy-start.11
  652.5 5.7 copy-start.12
  652.6 5.7 copy-start.13
  658.3 3.2 copy-start.6
  658.3 3.2 copy-start.9
  658.3 3.2 copy-start.10
  658.3 4.0 copy-start.14
  658.3 4.7 copy-start.15

commit v2 on v1

v2 whole, which is shorter than its diff:
```python
import functools

import jax
import jax.numpy as jnp
from jax import lax
from jax.experimental import pallas as pl
from jax.experimental.pallas import tpu as pltpu
from jax.sharding import PartitionSpec as P

F32, BF16 = jnp.float32, jnp.bfloat16
NAMES = ("w_gate", "w_up", "w_down")
BITS = (8, 4, 2)
DEVICES = 16
VMEM_LIMIT = 67_000_000


def adamw(w, m, v, g):
    m = 0.9 * m + 0.1 * g
    v = 0.95 * v + 0.05 * g * g
    step = m * lax.rsqrt(v + 1e-8) + 0.1 * w
    return (w - 0.02 * step).astype(BF16), m, v


def clipped(gradients, sum_of_squares, count):
    factor = jnp.minimum(1.0, 0.5 * lax.rsqrt(sum_of_squares / count + 1e-30))
    return [g * factor for g in gradients]


def thirds(columns):
    tiles, start, out = columns // 128, 0, []
    for k in range(3):
        size = 128 * (tiles // 3 + (k < tiles % 3))
        out.append((start, size))
        start += size
    return out


class Place:
    def __init__(self):
        me = self.me = lax.axis_index("dp")
        self.core = me % 2
        self.at = (me // 8, (me // 4) % 2, (me // 2) % 2)
        self.near = tuple(me + bit * (1 - 2 * v) for bit, v in zip(BITS, self.at))
        self.twin = me + 1 - 2 * self.core

    def greet(self, everyone):
        barrier = pltpu.get_barrier_semaphore()
        others = [(self.me + k) % DEVICES for k in range(1, DEVICES)] if everyone else [*self.near, self.twin]
        for other in others:
            pl.semaphore_signal(barrier, inc=1, device_id={"dp": other}, device_id_type=pl.DeviceIdType.MESH)
        pl.semaphore_wait(barrier, len(others))


def remote(src, dst, send, recv, device):
    return pltpu.make_async_remote_copy(
        src_ref=src, dst_ref=dst, send_sem=send, recv_sem=recv, device_id={"dp": device}, device_id_type=pl.DeviceIdType.MESH
    )


class Gather:
    def __init__(self, place, own, full, send, recv, here):
        self.place, self.own, self.full, self.send, self.recv, self.here = place, own, full, send, recv, here
        self.cuts = thirds(own.shape[-1])

    def local(self):
        x, y, z = self.place.at
        return pltpu.make_async_copy(self.own, self.full.at[x, y, z, self.place.core], self.here)

    def copy(self, stage, k):
        order = [(k + j) % 3 for j in range(3)]
        at = list(self.place.at)
        for d in order[:stage]:
            at[d] = slice(None)
        columns = pl.ds(*self.cuts[k])
        region = self.full.at[(*at, self.place.core, slice(None), columns)]
        src = region if stage else self.own.at[:, columns]
        n = 3 * stage + k
        return remote(src, region, self.send.at[n], self.recv.at[n], self.place.near[order[stage]])

    def across(self):
        region = self.full.at[:, :, :, self.place.core]
        return remote(region, region, self.send.at[9], self.recv.at[9], self.place.twin)

    def act(self, j):
        if j == 0:
            self.local().start()
            for k in range(3):
                self.copy(0, k).start()
        elif j in (1, 2):
            if j == 1:
                self.local().wait()
            for k in range(3):
                self.copy(j - 1, k).wait_recv()
                self.copy(j, k).start()
        elif j == 3:
            for k in range(3):
                self.copy(2, k).wait_recv()
            self.across().start()
        else:
            self.across().wait_recv()
            for stage in range(3):
                for k in range(3):
                    self.copy(stage, k).wait_send()
            self.across().wait_send()


class Scatter:
    def __init__(self, place, partial, out, total, first, landed, send, recv, here):
        self.place, self.partial, self.out, self.total, self.first = place, partial, out, total, first
        self.landed, self.send, self.recv, self.here = landed, send, recv, here
        self.rows, self.columns = partial.shape[-2:]
        self.cuts = thirds(self.columns)
        self.strip = 16
        self.kept = total is None
        self.sums, self.half = (partial, (place.core,)) if self.kept else (total, ())

    def load(self):
        return pltpu.make_async_copy(self.partial.at[:, :, :, self.place.core], self.total, self.here)

    def across(self):
        return remote(self.partial.at[:, :, :, 1 - self.place.core], self.first, self.send.at[9], self.recv.at[9], self.place.twin)

    def where(self, stage, k, keep):
        order = [(k + j) % 3 for j in range(3)]
        at = [slice(None)] * 3
        for d in order[:stage]:
            at[d] = self.place.at[d]
        d = order[stage]
        at[d] = self.place.at[d] if keep else 1 - self.place.at[d]
        return at, d

    def copy(self, stage, k):
        at, d = self.where(stage, k, False)
        n = 3 * stage + k
        src = self.sums.at[(*at, *self.half, slice(None), pl.ds(*self.cuts[k]))]
        return remote(src, self.landed[n], self.send.at[n], self.recv.at[n], self.place.near[d])

    def add_first(self):
        @pl.loop(0, 8)
        def _(block):
            at = (block // 4, (block // 2) % 2, block % 2)

            @pl.loop(0, self.rows // self.strip)
            def _(strip):
                rest = (pl.ds(strip * self.strip, self.strip), slice(None))
                to = (*at, *self.half, *rest)
                self.sums[to] = (self.sums[to].astype(F32) + self.first[(*at, *rest)].astype(F32)).astype(BF16)

    def add(self, stage, k):
        at, _ = self.where(stage, k, True)
        landed, free = self.landed[3 * stage + k], [d for d in range(3) if isinstance(at[d], slice)]
        columns = pl.ds(*self.cuts[k])
        for number in range(2 ** len(free)):
            bits = [(number >> b) & 1 for b in reversed(range(len(free)))]
            spot = list(at)
            for d, bit in zip(free, bits):
                spot[d] = bit

            @pl.loop(0, self.rows // self.strip)
            def _(strip, spot=spot, bits=bits):
                rows = pl.ds(strip * self.strip, self.strip)
                to = (*spot, *self.half, rows, columns)
                value = (self.sums[to].astype(F32) + landed[(*bits, rows, slice(None))].astype(F32)).astype(BF16)
                if stage < 2:
                    self.sums[to] = value
                else:
                    self.out[rows, columns] = value

    def act(self, j):
        if j == 0:
            self.across().start()
            if not self.kept:
                self.load().start()
        elif j == 1:
            if not self.kept:
                self.load().wait()
            self.across().wait_recv()
            self.add_first()
            for k in range(3):
                self.copy(0, k).start()
        elif j in (2, 3):
            for k in range(3):
                self.copy(j - 2, k).wait_recv()
                self.add(j - 2, k)
                self.copy(j - 1, k).start()
        else:
            for k in range(3):
                self.copy(2, k).wait_recv()
                self.add(2, k)
            for stage in range(3):
                for k in range(3):
                    self.copy(stage, k).wait_send()
            self.across().wait_send()


def scatter_scratch(rows, columns, kept=False):
    landed = [pltpu.VMEM((2,) * (2 - stage) + (rows, size), BF16) for stage in range(3) for _, size in thirds(columns)]
    half = pltpu.VMEM((2, 2, 2, rows, columns), BF16)
    mine = pltpu.VMEM((2, 2, 2, 2, rows, columns), BF16) if kept else half
    return [mine, half, *landed, pltpu.SemaphoreType.DMA((10,)), pltpu.SemaphoreType.DMA((10,)), pltpu.SemaphoreType.DMA]


class Norm:
    def __init__(self, place, own, all_of, out, send, recv):
        self.place, self.own, self.all_of, self.out, self.send, self.recv = place, own, all_of, out, send, recv

    def exchange(self):
        me, others = self.place.me, [(self.place.me + k) % DEVICES for k in range(1, DEVICES)]
        copies = [remote(self.own, self.all_of.at[me], self.send.at[k], self.recv.at[me], other) for k, other in enumerate(others)]
        for copy in copies:
            copy.start()
        self.all_of[me] = self.own[...]
        for k, other in enumerate(others):
            remote(self.own, self.all_of.at[other], self.send.at[k], self.recv.at[other], other).wait_recv()
        for copy in copies:
            copy.wait_send()
        total = self.all_of[0]
        for k in range(1, DEVICES):
            total = total + self.all_of[k]
        self.out[...] = total


ANY = pl.BlockSpec(memory_space=pl.ANY)


def once(shape):
    return pl.BlockSpec(shape, lambda i: (0,) * len(shape), pipeline_mode=pl.Buffered(1))


def fused(name, cid, steps, body, ins, in_specs, outs, out_specs, scratch, gathers=(), scatters=(), kept=(), norm_of=(), see=False, prelude=None):
    n_in, n_out = len(ins), len(outs)
    ng, ns, nk, nn = len(gathers), len(scatters), len(kept), len(norm_of)
    in_specs, ins, outs, out_specs = list(in_specs), list(ins), list(outs), list(out_specs)
    scratch = list(scratch)
    n_scratch = len(scratch)
    for w, layer, _ in gathers:
        r, c = w.shape[1:]
        ins.append(w)
        in_specs.append(pl.BlockSpec((1, r, c), lambda i, layer=layer: (layer, 0, 0), pipeline_mode=pl.Buffered(1)))
        outs.append(jax.ShapeDtypeStruct((2, 2, 2, 2, r, c), BF16))
        out_specs.append(ANY)
        scratch += [pltpu.SemaphoreType.DMA((10,)), pltpu.SemaphoreType.DMA((10,)), pltpu.SemaphoreType.DMA]
    for d, _ in scatters:
        ins.append(d)
        in_specs.append(ANY)
    for r, c in [d.shape[-2:] for d, _ in scatters] + [k[:2] for k in kept]:
        outs.append(jax.ShapeDtypeStruct((r, c), BF16))
        out_specs.append(pl.BlockSpec((r, c), lambda i: (0, 0), pipeline_mode=pl.Buffered(1)))
    for d, _ in scatters:
        scratch += scatter_scratch(*d.shape[-2:])
    for r, c, _ in kept:
        scratch += scatter_scratch(r, c, True)
    for g in norm_of:
        ins.append(g)
        in_specs.append(once(g.shape))
    if nn:
        outs.append(jax.ShapeDtypeStruct((8, 128), F32))
        out_specs.append(once((8, 128)))
        scratch += [pltpu.VMEM((8, 128), F32), pltpu.VMEM((DEVICES, 8, 128), F32)]
        scratch += [pltpu.SemaphoreType.DMA((DEVICES,)), pltpu.SemaphoreType.DMA((DEVICES,))]

    def kernel(*refs):
        refs = list(refs)

        def take(n):
            taken, refs[:n] = refs[:n], []
            return taken

        body_in, own, partial, known = take(n_in), take(ng), take(ns), take(nn)
        body_out, full, mine, sum_out = take(n_out), take(ng), take(ns + nk), take(1 if nn else 0)
        own_scratch = take(n_scratch)
        place = Place()
        exchanges = [(Gather(place, own[g].at[0], full[g], *take(3)), gathers[g][2]) for g in range(ng)]
        for s in range(ns):
            got = take(14)
            exchanges.append((Scatter(place, partial[s], mine[s], got[0], got[1], got[2:11], *got[11:]), scatters[s][1]))
        for k in range(nk):
            got = take(14)
            own_scratch.append(got[0])
            exchanges.append((Scatter(place, got[0], mine[ns + k], None, got[1], got[2:11], *got[11:]), kept[k][2]))
        step = pl.program_id(0)
        acts = sorted([(at, n, j) for n, (_, when) in enumerate(exchanges) for j, at in enumerate(when)] + [(0.05, -1, 0)] * bool(prelude))

        def due(place_of):
            for at, n, j in acts:
                if int(at) == place_of:
                    if n < 0:
                        prelude(*body_in, *body_out)
                    else:
                        exchanges[n][0].act(j)

        for at in sorted({int(at) for at, _, _ in acts if at < steps} | {0}):

            @pl.when(step == at)
            def _(at=at):
                if at == 0:
                    place.greet(bool(nn))
                due(at)

        body(step, *body_in, *body_out, *own_scratch, *(full if see else ()))

        @pl.when(step == steps - 1)
        def _():
            due(steps)
            if nn:
                one = sum(squares(ref) for ref in (*known, *mine))
                norm = Norm(place, *take(1), *take(1), sum_out[0], *take(2))
                norm.own[...] = jnp.full((8, 128), one, F32)
                norm.exchange()

    return pl.pallas_call(
        kernel,
        grid=(steps,),
        in_specs=in_specs,
        out_specs=out_specs,
        out_shape=outs,
        scratch_shapes=scratch,
        name=name,
        compiler_params=pltpu.CompilerParams(
            dimension_semantics=("arbitrary",), collective_id=cid, has_side_effects=True, vmem_limit_bytes=VMEM_LIMIT
        ),
    )(*ins)


def squares(ref):
    rows, columns = ref.shape

    def strip(s, total):
        part = ref[pl.ds(s * 16, 16), :].astype(F32)
        part = part * part
        return total + sum(part[:, c : c + 128] for c in range(0, columns, 128))

    return jnp.sum(lax.fori_loop(0, rows // 16, strip, jnp.zeros((16, 128), F32)))


def dot(a, b, contract=(1, 0)):
    return lax.dot_general(a, b, (((contract[0],), (contract[1],)), ((), ())), preferred_element_type=F32)


CHUNK = 512


def chunks(tokens, do, unroll=True):
    @pl.loop(0, tokens // CHUNK, unroll=unroll)
    def _(m):
        do(pl.ds(pl.multiple_of(m * CHUNK, CHUNK), CHUNK))


def strips(tokens, do):
    @pl.loop(0, tokens // 64)
    def _(m):
        do(pl.ds(pl.multiple_of(m * 64, 64), 64))


def normed(h):
    wide = h.astype(F32)
    return (wide * lax.rsqrt(jnp.mean(wide**2, -1, keepdims=True) + 1e-6)).astype(BF16)


def normed_back(h, by_a):
    wide, by_a = h.astype(F32), by_a.astype(F32)
    scale = lax.rsqrt(jnp.mean(wide**2, -1, keepdims=True) + 1e-6)
    return (by_a * scale - wide * (scale * scale * scale * jnp.mean(by_a * wide, -1, keepdims=True))).astype(BF16)


def forward_prelude(x, a, *_):
    def do(rows):
        a[rows, :] = normed(x[rows, :])

    strips(x.shape[0], do)


def forward_body(tiles, step, x, a, gate, up, h, a_next, hidden, w, wd, w_sem, wd_sem, g_full, u_full, d_full, *_):
    width = gate.shape[1]

    def copy(t, slot, m):
        columns = pl.ds(pl.multiple_of(t * width, width), width)
        return pltpu.make_async_copy((g_full, u_full)[m].at[:, :, :, :, :, columns], w.at[slot, m], w_sem.at[slot, m])

    @pl.when((step >= 1) & (step <= tiles))
    def _():
        t = step - 1
        slot = t % 2

        @pl.when(t == 0)
        def _():
            for m in range(2):
                copy(t, slot, m).start()

        @pl.when(t + 1 < tiles)
        def _():
            for m in range(2):
                copy(t + 1, 1 - slot, m).start()

        for m in range(2):
            copy(t, slot, m).wait()
        columns = pl.ds(pl.multiple_of(t * width, width), width)

        def do(rows):
            g = dot(a[rows, :], w[slot, 0].reshape(-1, width))
            u = dot(a[rows, :], w[slot, 1].reshape(-1, width))
            gate[rows, :], up[rows, :] = g, u
            hidden[rows, columns] = (g * jax.nn.sigmoid(g) * u).astype(BF16)

        chunks(a.shape[0], do)

    @pl.when(step == tiles + 1)
    def _():
        pltpu.make_async_copy(d_full, wd, wd_sem).start()
        pltpu.make_async_copy(d_full, wd, wd_sem).wait()

    @pl.when(step > tiles)
    def _():
        height = h.shape[0]
        rows = pl.ds(pl.multiple_of((step - tiles - 1) * height, height), height)
        out = dot(hidden[rows, :], wd[...].reshape(-1, wd.shape[-1])).astype(BF16).astype(F32)
        new = (x[rows, :].astype(F32) + out).astype(BF16)
        h[...] = new
        a_next[...] = normed(new)


def forward_last_body(step, a, wg, wu, dy, gate, up, dwd, hidden):
    def do(rows):
        g, u = dot(a[rows, :], wg[...]), dot(a[rows, :], wu[...])
        gate[rows, :], up[rows, :] = g, u
        hidden[rows, :] = (g * jax.nn.sigmoid(g) * u).astype(BF16)

    chunks(a.shape[0], do)
    dwd[...] = dot(hidden[...], dy[...], (0, 0)).astype(BF16)


def through_gate(dy, wd, gate, up, dgate, dup, hidden, rows):
    by_hidden = dot(dy[rows, :], wd[...], (1, 1)).astype(BF16).astype(F32)
    g, u = gate[rows, :], up[rows, :]
    s = jax.nn.sigmoid(g)
    silu = g * s
    dup[rows, :] = (by_hidden * silu).astype(BF16)
    dgate[rows, :] = (by_hidden * u * (s + silu * (1.0 - s))).astype(BF16)
    if hidden is not None:
        hidden[rows, :] = (silu * u).astype(BF16)


def turn(a, at):
    for m in range(a.shape[0] // 256):
        at[:, m * 256 : (m + 1) * 256] = a[m * 256 : (m + 1) * 256, :].T


def back_last_body(step, dy, wd, gate, up, a, dgate, dup, dwg, at):
    @pl.when(step == 0)
    def _():
        turn(a, at)

    chunks(a.shape[0], lambda rows: through_gate(dy, wd, gate, up, dgate, dup, None, rows))
    dwg[...] = dot(at[...], dgate[...]).astype(BF16)


def by_input_body(last, step, dgate, dup, wg, wu, h, dy, at, by_h, dwu, total):
    @pl.when(step == 0)
    def _():
        total[...] = jnp.zeros_like(total)

    def do(rows):
        total[rows, :] += dot(dgate[rows, :], wg[...], (1, 1)) + dot(dup[rows, :], wu[...], (1, 1))

    chunks(dgate.shape[0], do)
    dwu[...] = dot(at[...], dup[...]).astype(BF16)

    @pl.when(step == last)
    def _():
        def finish(rows):
            by_norm = normed_back(h[rows, :], total[rows, :].astype(BF16))
            by_h[rows, :] = (dy[rows, :].astype(F32) + by_norm.astype(F32)).astype(BF16)

        strips(dgate.shape[0], finish)


def back_first_body(step, dy, wd, gate, up, dgate, dup, dwd, hidden):
    chunks(dy.shape[0], lambda rows: through_gate(dy, wd, gate, up, dgate, dup, hidden, rows))
    dwd[...] = dot(hidden[...], dy[...], (0, 0)).astype(BF16)


def weights_body(half, step, a, dgate, dup, at, dwg, dwu):
    @pl.when(step == 0)
    def _():
        turn(a, at)

    for number, (d, dw) in enumerate(((dgate, dwg), (dup, dwu))):

        @pl.when(step // half == number)
        def _(d=d, dw=dw, number=number):
            width = d.shape[1]
            columns = pl.ds(pl.multiple_of((step - number * half) * width, width), width)
            dw[:, :, :, :, :, columns] = dot(at[...], d[...]).astype(BF16).reshape(*dw.shape[:5], width)


def solution(mesh):
    def step(x, dy, *arrays):
        weights, m, v = (arrays[i : i + 3] for i in (0, 3, 6))
        w_gate, w_up, w_down = weights
        x, dy = x[0], dy[0]
        tokens, d = x.shape
        ff = w_gate.shape[-1]
        tile = 256
        n = ff // tile

        def of(shape, dtype=BF16):
            return jax.ShapeDtypeStruct(shape, dtype)

        def columns(rows, width=tile):
            return pl.BlockSpec((rows, width), lambda i: (0, i))

        def rows_of(width, height=tile):
            return pl.BlockSpec((height, width), lambda i: (i, 0))

        def flat(full):
            return full.reshape(-1, full.shape[-1])

        def blocks(dw):
            return dw.reshape(2, 2, 2, 2, dw.shape[0] // 16, dw.shape[1])

        here = once((tokens, d))
        states = [of((tokens, ff), F32)] * 2
        halves = [of((tokens, ff))] * 2
        height = 256
        parts = tokens // height
        last = 1 + n + parts

        def tiles_of(i):
            return (0, jnp.clip(i - 1, 0, n - 1))

        def parts_of(i):
            return (jnp.clip(i - 1 - n, 0, parts - 1), 0)

        a0, gate0, up0, h1, a1, _, _, d0, g1, u1 = fused(
            "forward0", 2, last, functools.partial(forward_body, n), [x], [here],
            [of((tokens, d)), *states, of((tokens, d)), of((tokens, d))],
            [here, *[pl.BlockSpec((tokens, tile), tiles_of)] * 2, *[pl.BlockSpec((height, d), parts_of)] * 2],
            [
                pltpu.VMEM((tokens, ff), BF16), pltpu.VMEM((2, 2, 2, 2, 2, 2, d // DEVICES, tile), BF16),
                pltpu.VMEM((2, 2, 2, 2, ff // DEVICES, d), BF16), pltpu.SemaphoreType.DMA((2, 2)), pltpu.SemaphoreType.DMA,
            ],
            gathers=[
                (w_gate, 0, (0, 0.10, 0.20, 0.30, 0.50)),
                (w_up, 0, (0, 0.11, 0.21, 0.40, 0.51)),
                (w_down, 0, (0.22, 0.60, 6, 14, n + 1)),
                (w_gate, 1, (0.23, 0.61, 12, n + 7, last + 0.4)),
                (w_up, 1, (0.24, 6.5, n + 1.5, last + 0.1, last + 0.5)),
            ],
            see=True, prelude=forward_prelude,
        )
        d0 = flat(d0)
        g1, u1 = map(flat, (g1, u1))
        gate1, up1, dwd1, d1 = fused(
            "forward1", 3, n, forward_last_body,
            [a1, g1, u1, dy], [here, columns(d), columns(d), here],
            [*states, of((ff, d))], [columns(tokens), columns(tokens), rows_of(d)],
            [pltpu.VMEM((tokens, tile), BF16)],
            gathers=[(w_down, 1, (0, 2, 5, 10, 14))],
        )
        d1 = flat(d1)
        dgate1, dup1, dwg1, a1_t, sd1 = fused(
            "back1", 4, n, back_last_body,
            [dy, d1, gate1, up1, a1], [here, rows_of(d), columns(tokens), columns(tokens), here],
            [*halves, of((d, ff)), of((d, tokens))], [columns(tokens), columns(tokens), columns(d), once((d, tokens))],
            [],
            scatters=[(blocks(dwd1), (0, 3, 9, 12, 15))],
        )
        by_h, dwu1, sg1 = fused(
            "by_input1", 5, n, functools.partial(by_input_body, n - 1),
            [dgate1, dup1, g1, u1, h1, dy, a1_t],
            [columns(tokens), columns(tokens), columns(d), columns(d), here, here, once((d, tokens))],
            [of((tokens, d)), of((d, ff))], [here, columns(d)],
            [pltpu.VMEM((tokens, d), F32)],
            scatters=[(blocks(dwg1), (0, 3, 8, 11, 13))],
        )
        dgate0, dup0, dwd0, su1 = fused(
            "back0", 6, n, back_first_body,
            [by_h, d0, gate0, up0], [here, rows_of(d), columns(tokens), columns(tokens)],
            [*halves, of((ff, d))], [columns(tokens), columns(tokens), rows_of(d)],
            [pltpu.VMEM((tokens, tile), BF16)],
            scatters=[(blocks(dwu1), (0, 3, 9, 12, 15))],
        )
        sd0, sg0, su0, squares_sum = fused(
            "finish", 7, 2 * n, functools.partial(weights_body, n),
            [a0, dgate0, dup0],
            [
                here,
                pl.BlockSpec((tokens, tile), lambda i: (0, jnp.minimum(i, n - 1))),
                pl.BlockSpec((tokens, tile), lambda i: (0, jnp.maximum(i - n, 0))),
            ],
            [], [], [pltpu.VMEM((d, tokens), BF16)],
            scatters=[(blocks(dwd0), (0, 8, 22, 30, 2 * n + 0.1))],
            kept=[
                (d // 16, ff, (n, 25, 2 * n + 0.2, 2 * n + 0.4, 2 * n + 0.6)),
                (d // 16, ff, (2 * n, 2 * n + 0.05, 2 * n + 0.5, 2 * n + 0.7, 2 * n + 0.8)),
            ],
            norm_of=[sg1, su1, sd1],
        )
        gradients = [jnp.stack(pair).astype(F32) for pair in ((sg0, sg1), (su0, su1), (sd0, sd1))]
        gradients = clipped(gradients, squares_sum[0, 0], DEVICES * sum(g.size for g in gradients))
        new = [adamw(w.astype(F32), m, v, g) for w, m, v, g in zip(weights, m, v, gradients, strict=True)]
        return tuple(one[which] for which in range(3) for one in new)

    states, cut = P(("rep", "dp"), None, None), P(None, "dp", None)
    return jax.shard_map(
        step,
        mesh=mesh,
        in_specs=(states, states) + (cut,) * 9,
        out_specs=(P("rep", "dp", None),) * 9,
        check_vma=False,
    )
```

time: 666 us -> 550 us (0.83)
  Pallas kernels: 585 us -> 533 us
  blocking collectives: 31.9 us -> 0 us
  other arithmetic: 40.4 us -> 12.4 us
    pallas_call x8 -> x6, Pallas kernels: 585 us -> 533 us  [fused(): pl.pallas_call(kernel, grid=(steps,), in_specs=in_specs, out_specs=out_sp...]
    psum x1 -> x0, blocking collectives: 31.9 us -> none  [step(): squares = lax.psum(sum((jnp.sum(g * g) for g in gradients)), 'dp')]
    reduce_sum x5 -> x0, other arithmetic: 17.9 us -> none  [the longest x2 8.25 us: normed(): scale = lax.rsqrt(jnp.mean(wide ** 2, -1, keepdims=True) + 1e-06)]
where the time goes in v2:
time: 550 us
  Pallas kernels  533 us (97%)
  other arithmetic  12.4 us (2%)
    pallas_call x6, Pallas kernels, fused(): pl.pallas_call(kernel, grid=(steps,), in_specs=in_specs, out_specs=out_sp...  533 us
    convert_element_type x2, other arithmetic, adamw(): return ((w - 0.02 * step).astype(BF16), m, v)  12.4 us

profile of v2, /device:TPU:0, one launch (start us, length us, event | category | flops | bytes accessed | tf_op | source)
XLA Modules:
  0.0 549.7 jit_solution(2997168034729748726)
XLA Ops:
  0.6 154.5 %forward0.1 = (bf16[2048,1024]{1,0:T(8,128)(2,1)}, f32[2048,4096]{1,0:T(8,128)}, f32[2048,4096]{1,0:T(8,128)}, bf16[2048,1024]{1,0:T(8,128)(2,1)}, bf16[2048,102...) custom-call(bf16[2048,1024]{1,0:T(8,128)(2,1)} %bitcast.30, ...), custom_call_target="tpu_custom_call" | custom-call | tf_op jit(solution)/shard_map/forward0/pallas_call | solution.py:311
  155.2 64.8 %forward1.1 = (f32[2048,4096]{1,0:T(8,128)}, f32[2048,4096]{1,0:T(8,128)}, bf16[4096,1024]{1,0:T(8,128)(2,1)}, bf16[2,2,2,2,256,1024]{5,4,3,2,1,0:T(8,128)(2,1)}) custom-call(bf16[2048,1024]{1,0:T(8,128)(2,1)} %get-tuple-element.38.refs_0_.refs_4_, bf16[1024,4096]{1,0:T(8,128)(2,1)} %bitcast.20, bf16[1024,4096]{1,0:T(8,128)(2,1)} %bitcast.22, ...), custom_call_target="tpu_custom_call" | custom-call | tf_op jit(solution)/shard_map/forward1/pallas_call | solution.py:311
  220.0 63.7 %back1.1 = (bf16[2048,4096]{1,0:T(8,128)(2,1)}, bf16[2048,4096]{1,0:T(8,128)(2,1)}, bf16[1024,4096]{1,0:T(8,128)(2,1)}, bf16[1024,2048]{1,0:T(8,128)(2,1)}, bf16[256,1024]{1,0:T(8,128)(2,1)}) custom-call(bf16[2048,1024]{1,0:T(8,128)(2,1)} %bitcast.18, bf16[4096,1024]{1,0:T(8,128)(2,1)} %bitcast.29, f32[2048,4096]{1,0:T(8,128)} %get-tuple-element.42.refs_2_, ...), custom_call_target="tpu_custom_call" | custom-call | tf_op jit(solution)/shard_map/back1/pallas_call | solution.py:311
  283.8 75.6 %by_input1.1 = (bf16[2048,1024]{1,0:T(8,128)(2,1)}, bf16[1024,4096]{1,0:T(8,128)(2,1)}, bf16[64,4096]{1,0:T(8,128)(2,1)}) custom-call(bf16[2048,4096]{1,0:T(8,128)(2,1)} %get-tuple-element.45.refs_0_, bf16[2048,4096]{1,0:T(8,128)(2,1)} %get-tuple-element.46.refs_1_, bf16[1024,4096]{1,0:T(8,128)(2,1)} %bitcast.21, bf16[1024,4096]{1,0:T(8,128)(2,1)} %bitcast.23, ...), custom_call_target="tpu_custom_call" | custom-call | tf_op jit(solution)/shard_map/by_input1/pallas_call | solution.py:311
  359.4 56.7 %back0.1 = (bf16[2048,4096]{1,0:T(8,128)(2,1)}, bf16[2048,4096]{1,0:T(8,128)(2,1)}, bf16[4096,1024]{1,0:T(8,128)(2,1)}, bf16[64,4096]{1,0:T(8,128)(2,1)}) custom-call(bf16[2048,1024]{1,0:T(8,128)(2,1)} %get-tuple-element.50.refs_0_, bf16[4096,1024]{1,0:T(8,128)(2,1)} %bitcast.26, f32[2048,4096]{1,0:T(8,128)} %get-tuple-element.52.refs_2_, ...), custom_call_target="tpu_custom_call" | custom-call | tf_op jit(solution)/shard_map/back0/pallas_call | solution.py:311
  416.1 117.4 %finish.1 = (bf16[256,1024]{1,0:T(8,128)(2,1)}, bf16[64,4096]{1,0:T(8,128)(2,1)}, bf16[64,4096]{1,0:T(8,128)(2,1)}, f32[8,128]{1,0:T(8,128)}) custom-call(bf16[2048,1024]{1,0:T(8,128)(2,1)} %get-tuple-element.37.refs_0_, bf16[2048,4096]{1,0:T(8,128)(2,1)} %get-tuple-element.55.refs_1_, bf16[2048,4096]{1,0:T(8,128)(2,1)} %get-tuple-element.56.refs_2_, ...), custom_call_target="tpu_custom_call" | custom-call | tf_op jit(solution)/shard_map/finish/pallas_call | solution.py:311
  533.5 1.2 slice.3
  535.4 0.0 copy-start
  535.4 0.0 copy-start.1
  535.4 0.0 copy-start.2
  535.5 0.0 copy-start.3
  535.5 0.0 copy-start.4
  535.5 0.0 copy-start.5
  535.5 0.0 copy-start.6
  535.5 0.0 copy-start.7
  535.5 6.3 %fusion.8 = (bf16[2,256,1024]{2,1,0:T(8,128)(2,1)}, f32[2,256,1024]{2,1,0:T(8,128)}, f32[2,256,1024]{2,1,0:T(8,128)}) fusion(bf16[2,256,1024]{2,1,0:T(8,128)(2,1)} %refs_4_.3, f32[]{:T(128)} %bitcast.12, bf16[1,256,1024]{2,1,0:T(8,128)(2,1)} %bitcast.31, bf16[1,256,1024]{2,1,0:T(8,128)(2,1)} %bitcast.36, f32[2,256,1024]{2,1,0:T(8,128)} %param.21, ...), kind=kLoop, calls=%fused_computation.17 | loop fusion | flops 10485760 | bytes 11534340 | tf_op jit(solution)/shard_map/convert_element_type | solution.py:21
  541.8 0.0 copy-done
  541.8 0.0 copy-done.1
  541.8 0.0 copy-done.2
  541.8 0.0 copy-done.3
  541.8 0.0 copy-done.4
  541.8 0.0 copy-done.5
  541.8 1.1 copy-done.6
  542.9 0.6 copy-done.7
  543.5 6.2 %fusion.2 = (bf16[2,64,4096]{2,1,0:T(8,128)(2,1)}, f32[2,64,4096]{2,1,0:T(8,128)}, f32[2,64,4096]{2,1,0:T(8,128)}, bf16[2,64,4096]{2,1,0:T(8,128)(2,1)}, f32[2,64,4096]{2,1,0:T(8,128)}, /*index=5*/f32[2,64,4096]{2,1,0:T(8,128)}) fusion(bf16[2,64,4096]{2,1,0:T(8,128)(2,1)S(1)} %copy-done, f32[]{:T(128)} %bitcast.12, bf16[1,64,4096]{2,1,0:T(8,128)(2,1)S(1)} %bitcast.32, ...), kind=kLoop, calls=%fused_computation.11 | loop fusion | flops 20971520 | bytes 23068676 | tf_op jit(solution)/shard_map/convert_element_type | solution.py:21
Async XLA Ops:
  535.4 6.4 %copy-start = (bf16[2,64,4096]{2,1,0:T(8,128)(2,1)S(1)}, bf16[2,64,4096]{2,1,0:T(8,128)(2,1)}, u32[]{:S(2)}) copy-start(bf16[2,64,4096]{2,1,0:T(8,128)(2,1)} %refs_4_.2) | copy-start | bytes 3145732
  535.4 6.4 %copy-start.1 = (bf16[2,64,4096]{2,1,0:T(8,128)(2,1)S(1)}, bf16[2,64,4096]{2,1,0:T(8,128)(2,1)}, u32[]{:S(2)}) copy-start(bf16[2,64,4096]{2,1,0:T(8,128)(2,1)} %refs_5_.1) | copy-start | bytes 3145732
  535.4 6.3 %copy-start.2 = (bf16[64,4096]{1,0:T(8,128)(2,1)S(1)}, bf16[64,4096]{1,0:T(8,128)(2,1)}, u32[]{:S(2)}) copy-start(bf16[64,4096]{1,0:T(8,128)(2,1)} %get-tuple-element.58.refs_4_) | copy-start | bytes 1572868
  535.5 6.3 %copy-start.3 = (bf16[64,4096]{1,0:T(8,128)(2,1)S(1)}, bf16[64,4096]{1,0:T(8,128)(2,1)}, u32[]{:S(2)}) copy-start(bf16[64,4096]{1,0:T(8,128)(2,1)} %get-tuple-element.59.refs_5_) | copy-start | bytes 1572868
  535.5 6.3 %copy-start.4 = (f32[2,64,4096]{2,1,0:T(8,128)S(1)}, f32[2,64,4096]{2,1,0:T(8,128)}, u32[]{:S(2)}) copy-start(f32[2,64,4096]{2,1,0:T(8,128)} %param.19) | copy-start | bytes 6291460
  535.5 6.3 %copy-start.5 = (f32[2,64,4096]{2,1,0:T(8,128)S(1)}, f32[2,64,4096]{2,1,0:T(8,128)}, u32[]{:S(2)}) copy-start(f32[2,64,4096]{2,1,0:T(8,128)} %param.16) | copy-start | bytes 6291460
  535.5 7.5 %copy-start.6 = (f32[2,64,4096]{2,1,0:T(8,128)S(1)}, f32[2,64,4096]{2,1,0:T(8,128)}, u32[]{:S(2)}) copy-start(f32[2,64,4096]{2,1,0:T(8,128)} %param.20) | copy-start | bytes 6291460
  535.5 8.0 %copy-start.7 = (f32[2,64,4096]{2,1,0:T(8,128)S(1)}, f32[2,64,4096]{2,1,0:T(8,128)}, u32[]{:S(2)}) copy-start(f32[2,64,4096]{2,1,0:T(8,128)} %param.17) | copy-start | bytes 6291460

commit v3 on v2

--- a/solution.py
+++ b/solution.py
@@ -111,11 +111,12 @@
         self.rows, self.columns = partial.shape[-2:]
         self.cuts = thirds(self.columns)
         self.strip = 16
-        self.kept = total is None
+        self.kept, self.paired = total is None, len(partial.shape) == 5
         self.sums, self.half = (partial, (place.core,)) if self.kept else (total, ())
 
     def load(self):
-        return pltpu.make_async_copy(self.partial.at[:, :, :, self.place.core], self.total, self.here)
+        mine = self.partial if self.paired else self.partial.at[:, :, :, self.place.core]
+        return pltpu.make_async_copy(mine, self.total, self.here)
 
     def across(self):
         return remote(self.partial.at[:, :, :, 1 - self.place.core], self.first, self.send.at[9], self.recv.at[9], self.place.twin)
@@ -168,14 +169,16 @@
 
     def act(self, j):
         if j == 0:
-            self.across().start()
+            if not self.paired:
+                self.across().start()
             if not self.kept:
                 self.load().start()
         elif j == 1:
             if not self.kept:
                 self.load().wait()
-            self.across().wait_recv()
-            self.add_first()
+            if not self.paired:
+                self.across().wait_recv()
+                self.add_first()
             for k in range(3):
                 self.copy(0, k).start()
         elif j in (2, 3):
@@ -190,14 +193,61 @@
             for stage in range(3):
                 for k in range(3):
                     self.copy(stage, k).wait_send()
-            self.across().wait_send()
-
-
-def scatter_scratch(rows, columns, kept=False):
+            if not self.paired:
+                self.across().wait_send()
+
+
+def scatter_scratch(rows, columns, kept=False, paired=False):
     landed = [pltpu.VMEM((2,) * (2 - stage) + (rows, size), BF16) for stage in range(3) for _, size in thirds(columns)]
     half = pltpu.VMEM((2, 2, 2, rows, columns), BF16)
     mine = pltpu.VMEM((2, 2, 2, 2, rows, columns), BF16) if kept else half
-    return [mine, half, *landed, pltpu.SemaphoreType.DMA((10,)), pltpu.SemaphoreType.DMA((10,)), pltpu.SemaphoreType.DMA]
+    return [mine, pltpu.VMEM((8, 128), BF16) if paired else half, *landed, pltpu.SemaphoreType.DMA((10,)), pltpu.SemaphoreType.DMA((10,)), pltpu.SemaphoreType.DMA]
+
+
+class Pair:
+    def __init__(self, place, steps, out, partial, landed, send, recv):
+        self.place, self.out, self.partial, self.landed, self.send, self.recv = place, out, partial, landed, send, recv
+        self.rows, self.columns = partial.shape[-2:]
+        self.steps, self.whole = steps, steps == DEVICES and self.rows * DEVICES > self.columns
+
+    def copy(self, number):
+        if self.whole:
+            block = (number // 8, (number // 4) % 2, (number // 2) % 2)
+            src, dst = self.partial.at[(*block, number % 2)], self.landed.at[block]
+        else:
+            width = self.columns // self.steps
+            columns = pl.ds(pl.multiple_of(number * width, width), width)
+            src = self.partial.at[:, :, :, 1 - self.place.core, :, columns]
+            dst = self.landed.at[:, :, :, :, columns]
+        return remote(src, dst, self.send.at[number], self.recv.at[number], self.place.twin)
+
+    def made(self, number):
+        if self.whole:
+
+            @pl.when(number % 2 != self.place.core)
+            def _():
+                self.copy(number).start()
+        else:
+            self.copy(number).start()
+
+    def finish(self):
+        if self.whole:
+            for n in range(DEVICES // 2):
+                self.copy(2 * n + 1 - self.place.core).wait_send()
+                self.copy(2 * n + self.place.core).wait_recv()
+        else:
+            for n in range(self.steps):
+                self.copy(n).wait()
+
+        @pl.loop(0, 8)
+        def _(n):
+            block = (n // 4, (n // 2) % 2, n % 2)
+
+            @pl.loop(0, self.rows // 16)
+            def _(strip):
+                rest = (pl.ds(strip * 16, 16), slice(None))
+                mine = self.partial[(*block, self.place.core, *rest)].astype(F32)
+                self.out[(*block, *rest)] = (mine + self.landed[(*block, *rest)].astype(F32)).astype(BF16)
 
 
 class Norm:
@@ -227,7 +277,7 @@
     return pl.BlockSpec(shape, lambda i: (0,) * len(shape), pipeline_mode=pl.Buffered(1))
 
 
-def fused(name, cid, steps, body, ins, in_specs, outs, out_specs, scratch, gathers=(), scatters=(), kept=(), norm_of=(), see=False, prelude=None):
+def fused(name, cid, steps, body, ins, in_specs, outs, out_specs, scratch, gathers=(), scatters=(), kept=(), norm_of=(), see=False, prelude=None, pair=None):
     n_in, n_out = len(ins), len(outs)
     ng, ns, nk, nn = len(gathers), len(scatters), len(kept), len(norm_of)
     in_specs, ins, outs, out_specs = list(in_specs), list(ins), list(outs), list(out_specs)
@@ -247,12 +297,19 @@
         outs.append(jax.ShapeDtypeStruct((r, c), BF16))
         out_specs.append(pl.BlockSpec((r, c), lambda i: (0, 0), pipeline_mode=pl.Buffered(1)))
     for d, _ in scatters:
-        scratch += scatter_scratch(*d.shape[-2:])
-    for r, c, _ in kept:
-        scratch += scatter_scratch(r, c, True)
+        scratch += scatter_scratch(*d.shape[-2:], paired=d.ndim == 5)
+    for r, c, whens in kept:
+        for _ in whens:
+            scratch += scatter_scratch(r, c // len(whens), True)
     for g in norm_of:
         ins.append(g)
         in_specs.append(once(g.shape))
+    if pair:
+        half = (2, 2, 2, *pair)
+        outs.append(jax.ShapeDtypeStruct(half, BF16))
+        out_specs.append(once(half))
+        scratch += [pltpu.VMEM((2, 2, 2, 2, *pair), BF16), pltpu.VMEM(half, BF16)]
+        scratch += [pltpu.SemaphoreType.DMA((steps,)), pltpu.SemaphoreType.DMA((steps,))]
     if nn:
         outs.append(jax.ShapeDtypeStruct((8, 128), F32))
         out_specs.append(once((8, 128)))
@@ -267,17 +324,25 @@
             return taken
 
         body_in, own, partial, known = take(n_in), take(ng), take(ns), take(nn)
-        body_out, full, mine, sum_out = take(n_out), take(ng), take(ns + nk), take(1 if nn else 0)
+        body_out, full, mine, sum_out = take(n_out), take(ng), take(ns + nk), take(1 if nn or pair else 0)
         own_scratch = take(n_scratch)
         place = Place()
         exchanges = [(Gather(place, own[g].at[0], full[g], *take(3)), gathers[g][2]) for g in range(ng)]
         for s in range(ns):
             got = take(14)
             exchanges.append((Scatter(place, partial[s], mine[s], got[0], got[1], got[2:11], *got[11:]), scatters[s][1]))
-        for k in range(nk):
-            got = take(14)
+        for (_, c, whens), out in zip(kept, mine[ns:]):
+            for k, when in enumerate(whens):
+                got, size = take(14), c // len(whens)
+                own_scratch.append(got[0])
+                piece = out.at[:, pl.ds(k * size, size)]
+                exchanges.append((Scatter(place, got[0], piece, None, got[1], got[2:11], *got[11:]), when))
+        if pair:
+            got = take(4)
             own_scratch.append(got[0])
-            exchanges.append((Scatter(place, got[0], mine[ns + k], None, got[1], got[2:11], *got[11:]), kept[k][2]))
+            twins = Pair(place, steps, sum_out[0], *got)
+        if nn:
+            norm = Norm(place, *take(1), *take(1), sum_out[0], *take(2))
         step = pl.program_id(0)
         acts = sorted([(at, n, j) for n, (_, when) in enumerate(exchanges) for j, at in enumerate(when)] + [(0.05, -1, 0)] * bool(prelude))
 
@@ -299,13 +364,21 @@
 
         body(step, *body_in, *body_out, *own_scratch, *(full if see else ()))
 
+        if pair:
+            twins.made(step)
+        if nn:
+
+            @pl.when(step == 2)
+            def _():
+                norm.own[...] = jnp.full((8, 128), sum(squares(ref) for ref in known), F32)
+
         @pl.when(step == steps - 1)
         def _():
             due(steps)
+            if pair:
+                twins.finish()
             if nn:
-                one = sum(squares(ref) for ref in (*known, *mine))
-                norm = Norm(place, *take(1), *take(1), sum_out[0], *take(2))
-                norm.own[...] = jnp.full((8, 128), one, F32)
+                norm.own[...] += jnp.full((8, 128), sum(squares(ref) for ref in mine), F32)
                 norm.exchange()
 
     return pl.pallas_call(
@@ -445,51 +518,64 @@
         at[:, m * 256 : (m + 1) * 256] = a[m * 256 : (m + 1) * 256, :].T
 
 
-def back_last_body(step, dy, wd, gate, up, a, dgate, dup, dwg, at):
+def back_last_body(step, dy, wd, gate, up, a, dgate, dup, dwu, at, dwg):
     @pl.when(step == 0)
     def _():
         turn(a, at)
 
     chunks(a.shape[0], lambda rows: through_gate(dy, wd, gate, up, dgate, dup, None, rows))
-    dwg[...] = dot(at[...], dgate[...]).astype(BF16)
-
-
-def by_input_body(last, step, dgate, dup, wg, wu, h, dy, at, by_h, dwu, total):
+    width = dgate.shape[1]
+    columns = pl.ds(pl.multiple_of(step * width, width), width)
+    dwg[:, :, :, :, :, columns] = dot(at[...], dgate[...]).astype(BF16).reshape(*dwg.shape[:5], width)
+    dwu[...] = dot(at[...], dup[...]).astype(BF16)
+
+
+def by_input_body(last, step, dgate, dup, wg, wu, h, dy, by_h, total, ends, sems):
+    def copies():
+        return [pltpu.make_async_copy(ref, ends.at[n], sems.at[n]) for n, ref in enumerate((h, dy))]
+
     @pl.when(step == 0)
     def _():
+        for copy in copies():
+            copy.start()
         total[...] = jnp.zeros_like(total)
 
     def do(rows):
         total[rows, :] += dot(dgate[rows, :], wg[...], (1, 1)) + dot(dup[rows, :], wu[...], (1, 1))
 
     chunks(dgate.shape[0], do)
-    dwu[...] = dot(at[...], dup[...]).astype(BF16)
 
     @pl.when(step == last)
     def _():
+        for copy in copies():
+            copy.wait()
+
         def finish(rows):
-            by_norm = normed_back(h[rows, :], total[rows, :].astype(BF16))
-            by_h[rows, :] = (dy[rows, :].astype(F32) + by_norm.astype(F32)).astype(BF16)
+            by_norm = normed_back(ends[0, rows, :], total[rows, :].astype(BF16))
+            by_h[rows, :] = (ends[1, rows, :].astype(F32) + by_norm.astype(F32)).astype(BF16)
 
         strips(dgate.shape[0], finish)
 
 
-def back_first_body(step, dy, wd, gate, up, dgate, dup, dwd, hidden):
+def back_first_body(step, dy, wd, gate, up, dgate, dup, hidden, dwd):
     chunks(dy.shape[0], lambda rows: through_gate(dy, wd, gate, up, dgate, dup, hidden, rows))
-    dwd[...] = dot(hidden[...], dy[...], (0, 0)).astype(BF16)
-
-
-def weights_body(half, step, a, dgate, dup, at, dwg, dwu):
+    block = (step // 8, (step // 4) % 2, (step // 2) % 2, step % 2)
+    dwd[(*block, slice(None), slice(None))] = dot(hidden[...], dy[...], (0, 0)).astype(BF16)
+
+
+def weights_body(half, step, a, dgate, dup, at, *dws):
     @pl.when(step == 0)
     def _():
         turn(a, at)
 
-    for number, (d, dw) in enumerate(((dgate, dwg), (dup, dwu))):
-
-        @pl.when(step // half == number)
+    steps = 2 * half // len(dws)
+    for number, dw in enumerate(dws):
+        d = dgate if 2 * number < len(dws) else dup
+
+        @pl.when(step // steps == number)
         def _(d=d, dw=dw, number=number):
             width = d.shape[1]
-            columns = pl.ds(pl.multiple_of((step - number * half) * width, width), width)
+            columns = pl.ds(pl.multiple_of((step - number * steps) * width, width), width)
             dw[:, :, :, :, :, columns] = dot(at[...], d[...]).astype(BF16).reshape(*dw.shape[:5], width)
 
 
@@ -558,30 +644,34 @@
             gathers=[(w_down, 1, (0, 2, 5, 10, 14))],
         )
         d1 = flat(d1)
-        dgate1, dup1, dwg1, a1_t, sd1 = fused(
+        dgate1, dup1, dwu1, sd1, dwg1 = fused(
             "back1", 4, n, back_last_body,
             [dy, d1, gate1, up1, a1], [here, rows_of(d), columns(tokens), columns(tokens), here],
-            [*halves, of((d, ff)), of((d, tokens))], [columns(tokens), columns(tokens), columns(d), once((d, tokens))],
-            [],
-            scatters=[(blocks(dwd1), (0, 3, 9, 12, 15))],
+            [*halves, of((d, ff))], [columns(tokens), columns(tokens), columns(d)],
+            [pltpu.VMEM((d, tokens), BF16)],
+            scatters=[(blocks(dwd1), (0, 3, 8, 11, 14))],
+            pair=(d // DEVICES, ff),
         )
-        by_h, dwu1, sg1 = fused(
-            "by_input1", 5, n, functools.partial(by_input_body, n - 1),
-            [dgate1, dup1, g1, u1, h1, dy, a1_t],
-            [columns(tokens), columns(tokens), columns(d), columns(d), here, here, once((d, tokens))],
-            [of((tokens, d)), of((d, ff))], [here, columns(d)],
-            [pltpu.VMEM((tokens, d), F32)],
-            scatters=[(blocks(dwg1), (0, 3, 8, 11, 13))],
+        wide = 512
+        by_h, sg1 = fused(
+            "by_input1", 5, ff // wide, functools.partial(by_input_body, ff // wide - 1),
+            [dgate1, dup1, g1, u1, h1, dy],
+            [*[columns(tokens, wide)] * 2, *[columns(d, wide)] * 2, ANY, ANY],
+            [of((tokens, d))], [here],
+            [pltpu.VMEM((tokens, d), F32), pltpu.VMEM((2, tokens, d), BF16), pltpu.SemaphoreType.DMA((2,))],
+            scatters=[(dwg1, (0, 0.1, 4, 6, 8))],
         )
-        dgate0, dup0, dwd0, su1 = fused(
+        dgate0, dup0, su1, dwd0 = fused(
             "back0", 6, n, back_first_body,
             [by_h, d0, gate0, up0], [here, rows_of(d), columns(tokens), columns(tokens)],
-            [*halves, of((ff, d))], [columns(tokens), columns(tokens), rows_of(d)],
+            halves, [columns(tokens), columns(tokens)],
             [pltpu.VMEM((tokens, tile), BF16)],
             scatters=[(blocks(dwu1), (0, 3, 9, 12, 15))],
+            pair=(ff // DEVICES, d),
         )
+        end = 2 * n
         sd0, sg0, su0, squares_sum = fused(
-            "finish", 7, 2 * n, functools.partial(weights_body, n),
+            "finish", 7, end, functools.partial(weights_body, n),
             [a0, dgate0, dup0],
             [
                 here,
@@ -589,10 +679,10 @@
                 pl.BlockSpec((tokens, tile), lambda i: (0, jnp.maximum(i - n, 0))),
             ],
             [], [], [pltpu.VMEM((d, tokens), BF16)],
-            scatters=[(blocks(dwd0), (0, 8, 22, 30, 2 * n + 0.1))],
+            scatters=[(dwd0, (0, 0.1, 14, 20.5, 29))],
             kept=[
-                (d // 16, ff, (n, 25, 2 * n + 0.2, 2 * n + 0.4, 2 * n + 0.6)),
-                (d // 16, ff, (2 * n, 2 * n + 0.05, 2 * n + 0.5, 2 * n + 0.7, 2 * n + 0.8)),
+                (d // DEVICES, ff, [(8, 14.5, 27, end + 0.15, end + 0.35), (16, 22, end + 0.05, end + 0.25, end + 0.45)]),
+                (d // DEVICES, ff, [(24, 30, end + 0.2, end + 0.4, end + 0.55), (end, end + 0.1, end + 0.3, end + 0.5, end + 0.6)]),
             ],
             norm_of=[sg1, su1, sd1],
         )

time: 550 us -> 543 us (0.987)
  Pallas kernels: 533 us -> 525 us
    pallas_call x6, Pallas kernels: 533 us -> 525 us  [fused(): pl.pallas_call(kernel, grid=(steps,), in_specs=in_specs, out_specs=out_sp...]
where the time goes in v3:
time: 543 us; the launch traced here: 542 us
  Pallas kernels  525 us (97%)
  other arithmetic  12.4 us (2%)
    pallas_call x6, Pallas kernels, fused(): pl.pallas_call(kernel, grid=(steps,), in_specs=in_specs, out_specs=out_sp...  525 us
    convert_element_type x2, other arithmetic, adamw(): return ((w - 0.02 * step).astype(BF16), m, v)  12.4 us

profile of v3, /device:TPU:0, one launch (start us, length us, event | category | flops | bytes accessed | tf_op | source)
XLA Modules:
  0.0 542.3 jit_solution(11473949871034312544)
XLA Ops:
  0.6 154.5 %forward0.1 = (bf16[2048,1024]{1,0:T(8,128)(2,1)}, f32[2048,4096]{1,0:T(8,128)}, f32[2048,4096]{1,0:T(8,128)}, bf16[2048,1024]{1,0:T(8,128)(2,1)}, bf16[2048,102...) custom-call(bf16[2048,1024]{1,0:T(8,128)(2,1)} %bitcast.26, ...), custom_call_target="tpu_custom_call" | custom-call | tf_op jit(solution)/shard_map/forward0/pallas_call | solution.py:384
  155.2 64.8 %forward1.1 = (f32[2048,4096]{1,0:T(8,128)}, f32[2048,4096]{1,0:T(8,128)}, bf16[4096,1024]{1,0:T(8,128)(2,1)}, bf16[2,2,2,2,256,1024]{5,4,3,2,1,0:T(8,128)(2,1)}) custom-call(bf16[2048,1024]{1,0:T(8,128)(2,1)} %get-tuple-element.37.refs_0_.refs_4_, bf16[1024,4096]{1,0:T(8,128)(2,1)} %bitcast.18, bf16[1024,4096]{1,0:T(8,128)(2,1)} %bitcast.20, ...), custom_call_target="tpu_custom_call" | custom-call | tf_op jit(solution)/shard_map/forward1/pallas_call | solution.py:384
  220.0 84.1 %back1.1 = (bf16[2048,4096]{1,0:T(8,128)(2,1)}, bf16[2048,4096]{1,0:T(8,128)(2,1)}, bf16[1024,4096]{1,0:T(8,128)(2,1)}, bf16[256,1024]{1,0:T(8,128)(2,1)}, bf16[2,2,2,64,4096]{4,3,2,1,0:T(8,128)(2,1)}) custom-call(bf16[2048,1024]{1,0:T(8,128)(2,1)} %bitcast.16, bf16[4096,1024]{1,0:T(8,128)(2,1)} %bitcast.25, f32[2048,4096]{1,0:T(8,128)} %get-tuple-element.41.refs_2_, ...), custom_call_target="tpu_custom_call" | custom-call | tf_op jit(solution)/shard_map/back1/pallas_call | solution.py:384
  304.1 53.5 %by_input1.1 = (bf16[2048,1024]{1,0:T(8,128)(2,1)}, bf16[64,4096]{1,0:T(8,128)(2,1)}) custom-call(bf16[2048,4096]{1,0:T(8,128)(2,1)} %get-tuple-element.44.refs_0_, bf16[2048,4096]{1,0:T(8,128)(2,1)} %get-tuple-element.45.refs_1_, bf16[1024,4096]{1,0:T(8,128)(2,1)} %bitcast.19, bf16[1024,4096]{1,0:T(8,128)(2,1)} %bitcast.21, ...), custom_call_target="tpu_custom_call" | custom-call | tf_op jit(solution)/shard_map/by_input1/pallas_call | solution.py:384
  357.6 62.8 %back0.1 = (bf16[2048,4096]{1,0:T(8,128)(2,1)}, bf16[2048,4096]{1,0:T(8,128)(2,1)}, bf16[64,4096]{1,0:T(8,128)(2,1)}, bf16[2,2,2,256,1024]{4,3,2,1,0:T(8,128)(2,1)}) custom-call(bf16[2048,1024]{1,0:T(8,128)(2,1)} %get-tuple-element.48.refs_0_, bf16[4096,1024]{1,0:T(8,128)(2,1)} %bitcast.22, f32[2048,4096]{1,0:T(8,128)} %get-tuple-element.50.refs_2_, ...), custom_call_target="tpu_custom_call" | custom-call | tf_op jit(solution)/shard_map/back0/pallas_call | solution.py:384
  420.5 105.7 %finish.1 = (bf16[256,1024]{1,0:T(8,128)(2,1)}, bf16[64,4096]{1,0:T(8,128)(2,1)}, bf16[64,4096]{1,0:T(8,128)(2,1)}, f32[8,128]{1,0:T(8,128)}) custom-call(bf16[2048,1024]{1,0:T(8,128)(2,1)} %get-tuple-element.36.refs_0_, bf16[2048,4096]{1,0:T(8,128)(2,1)} %get-tuple-element.53.refs_1_, bf16[2048,4096]{1,0:T(8,128)(2,1)} %get-tuple-element.54.refs_2_, ...), custom_call_target="tpu_custom_call" | custom-call | tf_op jit(solution)/shard_map/finish/pallas_call | solution.py:384
  526.2 1.2 slice.3
  528.0 0.0 copy-start
  528.1 0.0 copy-start.1
  528.1 0.0 copy-start.2
  528.1 0.0 copy-start.3
  528.1 0.0 copy-start.4
  528.1 0.0 copy-start.5
  528.1 0.0 copy-start.6
  528.1 0.0 copy-start.7
  528.1 6.3 %fusion.8 = (bf16[2,256,1024]{2,1,0:T(8,128)(2,1)}, f32[2,256,1024]{2,1,0:T(8,128)}, f32[2,256,1024]{2,1,0:T(8,128)}) fusion(bf16[2,256,1024]{2,1,0:T(8,128)(2,1)} %refs_4_.3, f32[]{:T(128)} %bitcast.10, bf16[1,256,1024]{2,1,0:T(8,128)(2,1)} %bitcast.28, bf16[1,256,1024]{2,1,0:T(8,128)(2,1)} %bitcast.32, f32[2,256,1024]{2,1,0:T(8,128)} %param.21, ...), kind=kLoop, calls=%fused_computation.17 | loop fusion | flops 10485760 | bytes 11534340 | tf_op jit(solution)/shard_map/convert_element_type | solution.py:21
  534.4 0.0 copy-done
  534.4 0.0 copy-done.1
  534.4 0.0 copy-done.2
  534.4 0.0 copy-done.3
  534.4 0.0 copy-done.4
  534.4 0.0 copy-done.5
  534.4 1.1 copy-done.6
  535.6 0.6 copy-done.7
  536.2 6.2 %fusion.2 = (bf16[2,64,4096]{2,1,0:T(8,128)(2,1)}, f32[2,64,4096]{2,1,0:T(8,128)}, f32[2,64,4096]{2,1,0:T(8,128)}, bf16[2,64,4096]{2,1,0:T(8,128)(2,1)}, f32[2,64,4096]{2,1,0:T(8,128)}, /*index=5*/f32[2,64,4096]{2,1,0:T(8,128)}) fusion(bf16[2,64,4096]{2,1,0:T(8,128)(2,1)S(1)} %copy-done, f32[]{:T(128)} %bitcast.10, bf16[1,64,4096]{2,1,0:T(8,128)(2,1)S(1)} %bitcast.27, ...), kind=kLoop, calls=%fused_computation.11 | loop fusion | flops 20971520 | bytes 23068676 | tf_op jit(solution)/shard_map/convert_element_type | solution.py:21
Async XLA Ops:
  528.0 6.4 %copy-start = (bf16[2,64,4096]{2,1,0:T(8,128)(2,1)S(1)}, bf16[2,64,4096]{2,1,0:T(8,128)(2,1)}, u32[]{:S(2)}) copy-start(bf16[2,64,4096]{2,1,0:T(8,128)(2,1)} %refs_4_.2) | copy-start | bytes 3145732
  528.1 6.4 %copy-start.1 = (bf16[2,64,4096]{2,1,0:T(8,128)(2,1)S(1)}, bf16[2,64,4096]{2,1,0:T(8,128)(2,1)}, u32[]{:S(2)}) copy-start(bf16[2,64,4096]{2,1,0:T(8,128)(2,1)} %refs_5_.1) | copy-start | bytes 3145732
  528.1 6.3 %copy-start.2 = (bf16[64,4096]{1,0:T(8,128)(2,1)S(1)}, bf16[64,4096]{1,0:T(8,128)(2,1)}, u32[]{:S(2)}) copy-start(bf16[64,4096]{1,0:T(8,128)(2,1)} %get-tuple-element.56.refs_4_) | copy-start | bytes 1572868
  528.1 6.3 %copy-start.3 = (bf16[64,4096]{1,0:T(8,128)(2,1)S(1)}, bf16[64,4096]{1,0:T(8,128)(2,1)}, u32[]{:S(2)}) copy-start(bf16[64,4096]{1,0:T(8,128)(2,1)} %get-tuple-element.57.refs_5_) | copy-start | bytes 1572868
  528.1 6.3 %copy-start.4 = (f32[2,64,4096]{2,1,0:T(8,128)S(1)}, f32[2,64,4096]{2,1,0:T(8,128)}, u32[]{:S(2)}) copy-start(f32[2,64,4096]{2,1,0:T(8,128)} %param.19) | copy-start | bytes 6291460
  528.1 6.3 %copy-start.5 = (f32[2,64,4096]{2,1,0:T(8,128)S(1)}, f32[2,64,4096]{2,1,0:T(8,128)}, u32[]{:S(2)}) copy-start(f32[2,64,4096]{2,1,0:T(8,128)} %param.16) | copy-start | bytes 6291460
  528.1 7.5 %copy-start.6 = (f32[2,64,4096]{2,1,0:T(8,128)S(1)}, f32[2,64,4096]{2,1,0:T(8,128)}, u32[]{:S(2)}) copy-start(f32[2,64,4096]{2,1,0:T(8,128)} %param.20) | copy-start | bytes 6291460
  528.1 8.0 %copy-start.7 = (f32[2,64,4096]{2,1,0:T(8,128)S(1)}, f32[2,64,4096]{2,1,0:T(8,128)}, u32[]{:S(2)}) copy-start(f32[2,64,4096]{2,1,0:T(8,128)} %param.17) | copy-start | bytes 6291460

commit v4 on v3

--- a/solution.py
+++ b/solution.py
@@ -679,10 +679,10 @@
                 pl.BlockSpec((tokens, tile), lambda i: (0, jnp.maximum(i - n, 0))),
             ],
             [], [], [pltpu.VMEM((d, tokens), BF16)],
-            scatters=[(dwd0, (0, 0.1, 14, 20.5, 29))],
+            scatters=[(dwd0, (0, 0.1, 13.5, 19.5, 27))],
             kept=[
-                (d // DEVICES, ff, [(8, 14.5, 27, end + 0.15, end + 0.35), (16, 22, end + 0.05, end + 0.25, end + 0.45)]),
-                (d // DEVICES, ff, [(24, 30, end + 0.2, end + 0.4, end + 0.55), (end, end + 0.1, end + 0.3, end + 0.5, end + 0.6)]),
+                (d // DEVICES, ff, [(8, 13.5, 25, 30, end + 0.35), (16, 21, end + 0.05, end + 0.25, end + 0.45)]),
+                (d // DEVICES, ff, [(24, 29, end + 0.2, end + 0.4, end + 0.55), (end, end + 0.1, end + 0.3, end + 0.5, end + 0.6)]),
             ],
             norm_of=[sg1, su1, sd1],
         )

time: 543 us -> 541 us (level)
  no operation moved by 1% of the time
where the time goes in v4:
time: 541 us
  Pallas kernels  524 us (97%)
  other arithmetic  12.4 us (2%)
    pallas_call x6, Pallas kernels, fused(): pl.pallas_call(kernel, grid=(steps,), in_specs=in_specs, out_specs=out_sp...  524 us
    convert_element_type x2, other arithmetic, adamw(): return ((w - 0.02 * step).astype(BF16), m, v)  12.4 us

profile of v4, /device:TPU:0, one launch (start us, length us, event | category | flops | bytes accessed | tf_op | source)
XLA Modules:
  0.0 541.0 jit_solution(8745106687586764357)
XLA Ops:
  0.6 154.5 %forward0.1 = (bf16[2048,1024]{1,0:T(8,128)(2,1)}, f32[2048,4096]{1,0:T(8,128)}, f32[2048,4096]{1,0:T(8,128)}, bf16[2048,1024]{1,0:T(8,128)(2,1)}, bf16[2048,102...) custom-call(bf16[2048,1024]{1,0:T(8,128)(2,1)} %bitcast.26, ...), custom_call_target="tpu_custom_call" | custom-call | tf_op jit(solution)/shard_map/forward0/pallas_call | solution.py:384
  155.2 64.8 %forward1.1 = (f32[2048,4096]{1,0:T(8,128)}, f32[2048,4096]{1,0:T(8,128)}, bf16[4096,1024]{1,0:T(8,128)(2,1)}, bf16[2,2,2,2,256,1024]{5,4,3,2,1,0:T(8,128)(2,1)}) custom-call(bf16[2048,1024]{1,0:T(8,128)(2,1)} %get-tuple-element.37.refs_0_.refs_4_, bf16[1024,4096]{1,0:T(8,128)(2,1)} %bitcast.18, bf16[1024,4096]{1,0:T(8,128)(2,1)} %bitcast.20, ...), custom_call_target="tpu_custom_call" | custom-call | tf_op jit(solution)/shard_map/forward1/pallas_call | solution.py:384
  220.0 84.1 %back1.1 = (bf16[2048,4096]{1,0:T(8,128)(2,1)}, bf16[2048,4096]{1,0:T(8,128)(2,1)}, bf16[1024,4096]{1,0:T(8,128)(2,1)}, bf16[256,1024]{1,0:T(8,128)(2,1)}, bf16[2,2,2,64,4096]{4,3,2,1,0:T(8,128)(2,1)}) custom-call(bf16[2048,1024]{1,0:T(8,128)(2,1)} %bitcast.16, bf16[4096,1024]{1,0:T(8,128)(2,1)} %bitcast.25, f32[2048,4096]{1,0:T(8,128)} %get-tuple-element.41.refs_2_, ...), custom_call_target="tpu_custom_call" | custom-call | tf_op jit(solution)/shard_map/back1/pallas_call | solution.py:384
  304.1 53.5 %by_input1.1 = (bf16[2048,1024]{1,0:T(8,128)(2,1)}, bf16[64,4096]{1,0:T(8,128)(2,1)}) custom-call(bf16[2048,4096]{1,0:T(8,128)(2,1)} %get-tuple-element.44.refs_0_, bf16[2048,4096]{1,0:T(8,128)(2,1)} %get-tuple-element.45.refs_1_, bf16[1024,4096]{1,0:T(8,128)(2,1)} %bitcast.19, bf16[1024,4096]{1,0:T(8,128)(2,1)} %bitcast.21, ...), custom_call_target="tpu_custom_call" | custom-call | tf_op jit(solution)/shard_map/by_input1/pallas_call | solution.py:384
  357.6 62.8 %back0.1 = (bf16[2048,4096]{1,0:T(8,128)(2,1)}, bf16[2048,4096]{1,0:T(8,128)(2,1)}, bf16[64,4096]{1,0:T(8,128)(2,1)}, bf16[2,2,2,256,1024]{4,3,2,1,0:T(8,128)(2,1)}) custom-call(bf16[2048,1024]{1,0:T(8,128)(2,1)} %get-tuple-element.48.refs_0_, bf16[4096,1024]{1,0:T(8,128)(2,1)} %bitcast.22, f32[2048,4096]{1,0:T(8,128)} %get-tuple-element.50.refs_2_, ...), custom_call_target="tpu_custom_call" | custom-call | tf_op jit(solution)/shard_map/back0/pallas_call | solution.py:384
  420.5 104.3 %finish.1 = (bf16[256,1024]{1,0:T(8,128)(2,1)}, bf16[64,4096]{1,0:T(8,128)(2,1)}, bf16[64,4096]{1,0:T(8,128)(2,1)}, f32[8,128]{1,0:T(8,128)}) custom-call(bf16[2048,1024]{1,0:T(8,128)(2,1)} %get-tuple-element.36.refs_0_, bf16[2048,4096]{1,0:T(8,128)(2,1)} %get-tuple-element.53.refs_1_, bf16[2048,4096]{1,0:T(8,128)(2,1)} %get-tuple-element.54.refs_2_, ...), custom_call_target="tpu_custom_call" | custom-call | tf_op jit(solution)/shard_map/finish/pallas_call | solution.py:384
  524.8 1.2 slice.3
  526.7 0.0 copy-start
  526.7 0.0 copy-start.1
  526.7 0.0 copy-start.2
  526.7 0.0 copy-start.3
  526.7 0.0 copy-start.4
  526.7 0.0 copy-start.5
  526.7 0.0 copy-start.6
  526.8 0.0 copy-start.7
  526.8 6.3 %fusion.8 = (bf16[2,256,1024]{2,1,0:T(8,128)(2,1)}, f32[2,256,1024]{2,1,0:T(8,128)}, f32[2,256,1024]{2,1,0:T(8,128)}) fusion(bf16[2,256,1024]{2,1,0:T(8,128)(2,1)} %refs_4_.3, f32[]{:T(128)} %bitcast.10, bf16[1,256,1024]{2,1,0:T(8,128)(2,1)} %bitcast.28, bf16[1,256,1024]{2,1,0:T(8,128)(2,1)} %bitcast.32, f32[2,256,1024]{2,1,0:T(8,128)} %param.21, ...), kind=kLoop, calls=%fused_computation.17 | loop fusion | flops 10485760 | bytes 11534340 | tf_op jit(solution)/shard_map/convert_element_type | solution.py:21
  533.0 0.0 copy-done
  533.0 0.0 copy-done.1
  533.1 0.0 copy-done.2
  533.1 0.0 copy-done.3
  533.1 0.0 copy-done.4
  533.1 0.0 copy-done.5
  533.1 1.1 copy-done.6
  534.2 0.6 copy-done.7
  534.8 6.2 %fusion.2 = (bf16[2,64,4096]{2,1,0:T(8,128)(2,1)}, f32[2,64,4096]{2,1,0:T(8,128)}, f32[2,64,4096]{2,1,0:T(8,128)}, bf16[2,64,4096]{2,1,0:T(8,128)(2,1)}, f32[2,64,4096]{2,1,0:T(8,128)}, /*index=5*/f32[2,64,4096]{2,1,0:T(8,128)}) fusion(bf16[2,64,4096]{2,1,0:T(8,128)(2,1)S(1)} %copy-done, f32[]{:T(128)} %bitcast.10, bf16[1,64,4096]{2,1,0:T(8,128)(2,1)S(1)} %bitcast.27, ...), kind=kLoop, calls=%fused_computation.11 | loop fusion | flops 20971520 | bytes 23068676 | tf_op jit(solution)/shard_map/convert_element_type | solution.py:21
Async XLA Ops:
  526.7 6.4 %copy-start = (bf16[2,64,4096]{2,1,0:T(8,128)(2,1)S(1)}, bf16[2,64,4096]{2,1,0:T(8,128)(2,1)}, u32[]{:S(2)}) copy-start(bf16[2,64,4096]{2,1,0:T(8,128)(2,1)} %refs_4_.2) | copy-start | bytes 3145732
  526.7 6.4 %copy-start.1 = (bf16[2,64,4096]{2,1,0:T(8,128)(2,1)S(1)}, bf16[2,64,4096]{2,1,0:T(8,128)(2,1)}, u32[]{:S(2)}) copy-start(bf16[2,64,4096]{2,1,0:T(8,128)(2,1)} %refs_5_.1) | copy-start | bytes 3145732
  526.7 6.3 %copy-start.2 = (bf16[64,4096]{1,0:T(8,128)(2,1)S(1)}, bf16[64,4096]{1,0:T(8,128)(2,1)}, u32[]{:S(2)}) copy-start(bf16[64,4096]{1,0:T(8,128)(2,1)} %get-tuple-element.56.refs_4_) | copy-start | bytes 1572868
  526.7 6.3 %copy-start.3 = (bf16[64,4096]{1,0:T(8,128)(2,1)S(1)}, bf16[64,4096]{1,0:T(8,128)(2,1)}, u32[]{:S(2)}) copy-start(bf16[64,4096]{1,0:T(8,128)(2,1)} %get-tuple-element.57.refs_5_) | copy-start | bytes 1572868
  526.7 6.3 %copy-start.4 = (f32[2,64,4096]{2,1,0:T(8,128)S(1)}, f32[2,64,4096]{2,1,0:T(8,128)}, u32[]{:S(2)}) copy-start(f32[2,64,4096]{2,1,0:T(8,128)} %param.19) | copy-start | bytes 6291460
  526.7 6.3 %copy-start.5 = (f32[2,64,4096]{2,1,0:T(8,128)S(1)}, f32[2,64,4096]{2,1,0:T(8,128)}, u32[]{:S(2)}) copy-start(f32[2,64,4096]{2,1,0:T(8,128)} %param.16) | copy-start | bytes 6291460
  526.7 7.5 %copy-start.6 = (f32[2,64,4096]{2,1,0:T(8,128)S(1)}, f32[2,64,4096]{2,1,0:T(8,128)}, u32[]{:S(2)}) copy-start(f32[2,64,4096]{2,1,0:T(8,128)} %param.20) | copy-start | bytes 6291460
  526.8 8.0 %copy-start.7 = (f32[2,64,4096]{2,1,0:T(8,128)S(1)}, f32[2,64,4096]{2,1,0:T(8,128)}, u32[]{:S(2)}) copy-start(f32[2,64,4096]{2,1,0:T(8,128)} %param.17) | copy-start | bytes 6291460
